TPU v7x, 64 devices: a 2x2x8 block of a 4x4x8 slice. The times are simulated.
64 devices in a mesh: dp: 4 (over x, y), fsdp: 16 (over z, core).
Axes of the slice: x: 2, y: 2, z: 8, core: 2. Of those that a mesh axis runs over, the one named last changes fastest.
The devices are a block of a 4x4x8 slice.
Arguments:
- tokens: int32 [64, 128], P(('dp', 'fsdp')), parts along dimension 0
- embed_table: bfloat16 [128256, 2048], P('fsdp')
- norm_attn: bfloat16 [2048], P('fsdp')
- w_qkv: bfloat16 [2048, 3072], P('fsdp')
- w_out: bfloat16 [2048, 2048], P('fsdp')
- norm_mlp: bfloat16 [2048], P('fsdp')
- w_gate_up: bfloat16 [2048, 16384], P('fsdp')
- w_down: bfloat16 [8192, 2048], P('fsdp')
- rope_scale: float32 [32], replicated
Outputs:
- output 1: bfloat16 [64, 128, 2048], P(('dp', 'fsdp')), parts along dimension 0
- output 2: bfloat16 [64, 128, 8, 64], P(('dp', 'fsdp')), parts along dimension 0
- output 3: bfloat16 [64, 128, 8, 64], P(('dp', 'fsdp')), parts along dimension 0
There are 4 independent parts. A program takes and returns all parts, laid end to end along the dimension named above; an argument that names none is the same for every part.
All inputs are finite; a program needn't handle non-finite values.
Results may differ from a plain program's by a relative error of at most 0.0117517.
Values are sent between devices in bfloat16 or wider.
A program may use at most 768 MiB of HBM per device.

v0:
```python
import functools
import math

import jax
import jax.numpy as jnp
from jax import lax
from jax.experimental import pallas as pl
from jax.experimental.pallas import tpu as pltpu
from jax.sharding import PartitionSpec as P

NORM_EPS = 1e-5
ROPE_THETA = 10000.0
PICK = 32
DEPTH = 4
LANES = 128
MESH = pl.DeviceIdType.MESH
BF16 = jnp.bfloat16
F32 = jnp.float32


def aligned(start, size, step):
    return pl.ds(pl.multiple_of(start, step), size)


class Where:
    def __init__(self, side, n_fsdp):
        self.side = side
        self.nz = n_fsdp // 2
        self.dp = lax.axis_index('dp')
        self.f = lax.axis_index('fsdp')
        self.z = self.f // 2
        self.c = self.f % 2
        self.px = self.dp // side
        self.py = self.dp % side
        self.me = 2 * (self.px % 2) + self.py % 2

    def chip(self, dz):
        return lax.rem(self.z + dz + self.nz, self.nz)

    def along_z(self, dz, core):
        return (self.dp, 2 * self.chip(dz) + core)

    def partner(self):
        return (self.dp, 2 * self.z + 1 - self.c)

    def square(self, rel, core):
        px = self.px + (1 - 2 * (self.px % 2)) if rel & 2 else self.px
        py = self.py + (1 - 2 * (self.py % 2)) if rel & 1 else self.py
        return (px * self.side + py, 2 * self.z + core)


def greet(devices):
    barrier = pltpu.get_barrier_semaphore()
    for dev in devices:
        pl.semaphore_signal(barrier, inc=1, device_id=dev, device_id_type=MESH)
    pl.semaphore_wait(barrier, len(devices))


def remote(src, dst, ssem, rsem, dev):
    return pltpu.make_async_remote_copy(src_ref=src, dst_ref=dst, send_sem=ssem, recv_sem=rsem, device_id=dev, device_id_type=MESH)


def arrived(ref, sem):
    pltpu.make_async_copy(ref, ref, sem).wait()


def ids_kernel(side, pc, tok_ref, gain_ref, w_qkv, w_out, w_gu, w_dn, ids_ref, gains_ref, pq_ref, pe_ref, pd_ref,
               pk, lsem, ssem, rsem, pack_sem, store_sem):
    n_fsdp = pc.n_fsdp
    w = Where(side, n_fsdp)
    pack_copies(pc, w.me, pk, w_qkv, w_out, w_gu, w_dn, pack_sem)
    greet([(w.dp, lax.rem(w.f + k, n_fsdp)) for k in range(1, n_fsdp)])
    own = [pltpu.make_async_copy(tok_ref, ids_ref.at[w.f], lsem.at[0]),
           pltpu.make_async_copy(gain_ref, gains_ref.at[w.f], lsem.at[1])]
    for cp in own:
        cp.start()
    sent = []
    for k in range(1, n_fsdp):
        dev = (w.dp, lax.rem(w.f + k, n_fsdp))
        for j, (src, dst) in enumerate(((tok_ref, ids_ref), (gain_ref, gains_ref))):
            cp = remote(src, dst.at[w.f], ssem.at[j, k], rsem.at[j, k], dev)
            cp.start()
            sent.append(cp)
    arrived(pk, pack_sem)
    lo = 0
    stores = []
    for j, ref in enumerate((pq_ref, pe_ref, pd_ref)):
        stores.append(pltpu.make_async_copy(pk.at[:, pl.ds(lo, ref.shape[1])], ref, store_sem.at[j]))
        stores[-1].start()
        lo += ref.shape[1]
    for cp in own + stores:
        cp.wait()
    for cp in sent:
        cp.wait_send()
    for k in range(1, n_fsdp):
        src = lax.rem(w.f - k + n_fsdp, n_fsdp)
        arrived(ids_ref.at[src], rsem.at[0, k])
        arrived(gains_ref.at[src], rsem.at[1, k])


class Pieces:
    def __init__(self, rows, q4, kv4, w4, f4, n_fsdp, width):
        self.rows = rows
        self.q4, self.kv4, self.w4, self.f4 = q4, kv4, w4, f4
        self.n_fsdp = n_fsdp
        self.width = width
        self.qkv = q4 + 2 * kv4
        self.gu0 = self.qkv + w4
        self.gu_w = 2 * f4 * n_fsdp // 4
        self.dn0 = self.gu0 + 4 * self.gu_w
        self.dn_w = width // 4
        self.total = self.dn0 + width
        self.late = self.total - self.qkv
        self.chunks = [(0, self.qkv), (self.qkv, w4)]
        self.chunks += [(self.gu0 + b * self.gu_w, self.gu_w) for b in range(4)]
        self.chunks += [(self.dn0 + n * self.dn_w, self.dn_w) for n in range(4)]
        self.early = 6


def pack_copies(pc, me, pk, w_qkv, w_out, w_gu, w_dn, sem):
    q4, kv4, w4, f4 = pc.q4, pc.kv4, pc.w4, pc.f4
    first = [
        (w_qkv.at[:, aligned(me * q4, q4, LANES)], pk.at[:, pl.ds(0, q4)]),
        (w_qkv.at[:, aligned(4 * q4 + me * kv4, kv4, LANES)], pk.at[:, pl.ds(q4, kv4)]),
        (w_qkv.at[:, aligned(4 * q4 + 4 * kv4 + me * kv4, kv4, LANES)], pk.at[:, pl.ds(q4 + kv4, kv4)]),
    ]
    for src, dst in first:
        pltpu.make_async_copy(src, dst, sem).start()
    pltpu.make_async_copy(w_out.at[:, aligned(me * w4, w4, LANES)], pk.at[:, pl.ds(pc.qkv, w4)], sem).start()
    ff = 4 * f4 * pc.n_fsdp
    for d in range(pc.n_fsdp):
        b, k = d // 4, d % 4
        for part in range(2):
            src = w_gu.at[:, aligned(part * ff + d * 4 * f4 + me * f4, f4, LANES)]
            dst = pk.at[:, pl.ds(pc.gu0 + b * pc.gu_w + part * (pc.gu_w // 2) + k * f4, f4)]
            pltpu.make_async_copy(src, dst, sem).start()
    pltpu.make_async_copy(w_dn.at[aligned(me * f4, f4, LANES), :], pk.at[:, pl.ds(pc.dn0, pc.width)], sem).start()


def gather_ids(side, pc, tokens, gains, w_qkv, w_out, w_gu, w_dn):
    n_fsdp = pc.n_fsdp
    vmem, hbm = pl.BlockSpec(memory_space=pltpu.VMEM), pl.BlockSpec(memory_space=pl.ANY)
    dma = pltpu.SemaphoreType.DMA
    return pl.pallas_call(
        functools.partial(ids_kernel, side, pc),
        out_shape=(
            jax.ShapeDtypeStruct((n_fsdp,) + tokens.shape, tokens.dtype),
            jax.ShapeDtypeStruct((n_fsdp,) + gains.shape, gains.dtype),
            jax.ShapeDtypeStruct((pc.rows, pc.qkv), BF16),
            jax.ShapeDtypeStruct((pc.rows, pc.dn0 - pc.qkv), BF16),
            jax.ShapeDtypeStruct((pc.rows, pc.width), BF16)),
        in_specs=[vmem, vmem, hbm, hbm, hbm, hbm],
        out_specs=(vmem, vmem, hbm, hbm, hbm),
        scratch_shapes=[pltpu.VMEM((pc.rows, pc.total), BF16), dma((2,)), dma((2, n_fsdp)), dma((2, n_fsdp)), dma, dma((3,))],
        compiler_params=pltpu.CompilerParams(collective_id=0, has_side_effects=True),
        name='ids',
    )(tokens, gains, w_qkv, w_out, w_gu, w_dn)


def gather_kernel(n_tok, gid_ref, tgt_ref, table_ref, out_ref, buf, sems):
    width = table_ref.shape[2]
    n_step = n_tok // PICK

    def fetch(step, slot):
        for i in range(PICK):
            pltpu.make_async_copy(table_ref.at[gid_ref[step * PICK + i]], buf.at[slot, i], sems.at[slot]).start()

    for j in range(DEPTH - 1):
        fetch(j, j)

    def body(step, carry):
        slot = lax.rem(step, DEPTH)

        @pl.when(step + DEPTH - 1 < n_step)
        def _():
            fetch(step + DEPTH - 1, lax.rem(step + DEPTH - 1, DEPTH))
        arrived(buf.at[slot], sems.at[slot])
        rows = aligned(step * PICK, PICK, PICK)
        hot = (lax.broadcasted_iota(jnp.int32, (PICK, PICK * 8), 1) == tgt_ref[rows, :]).astype(BF16)
        got = jnp.dot(hot, buf[slot].reshape(PICK * 8, width), preferred_element_type=F32)
        out_ref[rows, :] = got.astype(BF16)
        return carry
    lax.fori_loop(0, n_step, body, 0)


def gather_table(ids, owned, table):
    n_tok = ids.shape[0]
    n_rows, width = table.shape
    gid = jnp.where(owned, ids // 8, jnp.arange(n_tok, dtype=jnp.int32) % (n_rows // 8))
    place = jnp.arange(n_tok, dtype=jnp.int32) % PICK
    tgt = jnp.where(owned, 8 * place + ids % 8, -1)[:, None]
    return pl.pallas_call(
        functools.partial(gather_kernel, n_tok),
        out_shape=jax.ShapeDtypeStruct((n_tok, width), BF16),
        in_specs=[pl.BlockSpec(memory_space=pltpu.SMEM), pl.BlockSpec(memory_space=pltpu.VMEM), pl.BlockSpec(memory_space=pl.ANY)],
        out_specs=pl.BlockSpec(memory_space=pltpu.VMEM),
        scratch_shapes=[pltpu.VMEM((DEPTH, PICK, 8, width), BF16), pltpu.SemaphoreType.DMA((DEPTH,))],
        compiler_params=pltpu.CompilerParams(vmem_limit_bytes=48 * 2**20),
        cost_estimate=pl.CostEstimate(flops=80 * 10**9, bytes_accessed=9 * n_tok * width * 2, transcendentals=0),
        name='rows',
    )(gid, tgt, table.reshape(n_rows // 8, 8, width))


def embed_kernel(side, pc, rows_ref, pq_ref, n0_ref, n1_ref, pe_ref, pd_ref, f0_ref, f1_ref, xa_ref, xb_ref, q_ref, te_ref, td_ref, tf_ref,
                 got, peer, rp, sb, pk, xo,
                 got_sem, pack_sem, own_sem, d2d_s, d2d_r, f_s, f_r, push_s, push_r,
                 peer_s, peer_r, rs_s, rs_r, home_sem, x_s, x_r):
    n_fsdp = pc.n_fsdp
    w = Where(side, n_fsdp)
    nz = w.nz
    far = nz // 2
    seq = got.shape[2]
    hw = got.shape[3]
    width = 2 * hw
    order = [far]
    for o in range(far - 1, 0, -1):
        order += [o, -o]
    order += [0]
    mine = aligned(w.c * hw, hw, LANES)
    other = aligned((1 - w.c) * hw, hw, LANES)
    for k in range(len(order)):
        dest = w.chip(order[k])
        pltpu.make_async_copy(rows_ref.at[dest, :, :, mine], got.at[dest], got_sem.at[k]).start()
    for j, src in enumerate((pq_ref, n0_ref, n1_ref)):
        pltpu.make_async_copy(src, pk.at[j], pack_sem.at[j]).start()
    greet([w.partner()] + [w.along_z(dz, core) for dz in (1, -1) for core in (0, 1)] + [w.square(rel, core) for rel in (1, 2) for core in (0, 1)])
    dirs = (1, -1)

    for k in range(len(order)):
        dest = w.chip(order[k])
        remote(rows_ref.at[dest, :, :, other], peer.at[dest], peer_s.at[k], peer_r.at[k], w.partner()).start()

    here_q = (2 * w.z + w.c, 2 * w.chip(-1) + w.c, 2 * w.chip(1) + w.c)
    swaps = [(src, q_ref.at[here_q[j]]) for j, src in enumerate((pq_ref, n0_ref, n1_ref))]
    swaps += [(pe_ref, te_ref), (pd_ref, td_ref), (f0_ref, tf_ref.at[0]), (f1_ref, tf_ref.at[1])]
    own = [remote(src, dst, d2d_s.at[j], d2d_r.at[j], w.partner()) for j, (src, dst) in enumerate(swaps)]


    def pair(dz):
        return q_ref.at[pl.ds(2 * w.chip(dz), 2)]

    def single(dz, i):
        return q_ref.at[pl.ds(2 * w.chip(dz) + i, 1)]

    def push(ref, i, h):
        remote(ref, ref, push_s.at[i, h], push_r, w.partner()).start()

    local = []

    def forward(h):
        @pl.when(w.c == 1)
        def _():
            for i, dz in enumerate(dirs):
                if h == 1:
                    local[1 + i].wait()
                    own[1 + i].wait_recv()
                elif h < far:
                    arrived(pair(-dz * h), f_r.at[i, h])
                else:
                    arrived(single(-dz * h, i), f_r.at[i, h])
                if h < far - 1:
                    remote(pair(-dz * h), pair(-dz * h), f_s.at[i, h + 1], f_r.at[i, h + 1], w.along_z(dz, 1)).start()
                elif h == far - 1:
                    remote(single(-dz * h, i), single(-dz * h, i), f_s.at[i, h + 1], f_r.at[i, h + 1], w.along_z(dz, 1)).start()
                if h > 1:
                    push(pair(-dz * h) if h < far else single(-dz * h, i), i, h)

    def addto(dst, terms, q):
        def one(r, carry):
            rows = aligned(q * (seq // 2) + r * 32, 32, 32)
            val = terms[0](rows)
            for term in terms[1:]:
                val = val + term(rows)
            dst(rows, val)
            return carry
        lax.fori_loop(0, seq // 64, one, 0)

    def part(ref, q):
        return ref.at[pl.ds(q * (seq // 2), seq // 2)]

    def rs_stage(k, h):
        o = order[k]
        dest = w.chip(o)
        if h == 0:
            arrived(got.at[dest], got_sem.at[k])
            arrived(peer.at[dest], peer_r.at[k])
        if o == 0:
            return
        dist = abs(o)
        for i, dz in enumerate(dirs):
            if (o * dz < 0 and o != far) or (dist == far and h != i):
                continue
            for q in range(2):
                terms = [lambda r: got[dest, h, r, :], lambda r: peer[dest, h, r, :]]
                if dist < far - 1 or (dist == far - 1 and h == i):
                    arrived(part(rp.at[i, dist, h], q), rs_r.at[i, dist, h, q])
                    terms.append(lambda r, i=i: rp[i, dist, h, r, :])

                def put(r, val, i=i):
                    sb[i, dist - 1, h, r, :] = val
                addto(put, terms, q)
                remote(part(sb.at[i, dist - 1, h], q), part(rp.at[i, dist - 1, h], q), rs_s.at[i, dist - 1, h, q],
                       rs_r.at[i, dist - 1, h, q], w.along_z(dz, w.c)).start()

    def finish(h):
        for q in range(2):
            terms = [lambda r: got[w.z, h, r, :], lambda r: peer[w.z, h, r, :]]
            for i in range(2):
                arrived(part(rp.at[i, 0, h], q), rs_r.at[i, 0, h, q])
                terms.append(lambda r, i=i: rp[i, 0, h, r, :])

            def put(r, val):
                xo[h, r, :] = val
            addto(put, terms, q)
        dst = (xa_ref.at[0] if h == 0 else xb_ref).at[:, mine]

        @pl.when(w.c == 0)
        def _():
            pltpu.make_async_copy(xo.at[h], dst, home_sem.at[h]).start()

        @pl.when(w.c == 1)
        def _():
            remote(xo.at[h], dst, home_sem.at[h], x_r.at[0, h], w.partner()).start()

    sides = ((2, w.square(2, 0)), (1, w.square(1, 0)))
    spread = [remote(xo.at[0], xa_ref.at[rel, :, mine], x_s.at[j], x_r.at[rel, w.c], dev) for j, (rel, dev) in enumerate(sides)]
    col = [pl.ds(j * hw, hw) for j in range(2)]
    relay = [remote(xa_ref.at[rel, :, col[j]], xa_ref.at[3, :, col[j]], x_s.at[2 + j], x_r.at[3, j], sides[1 - j][1]) for j, (rel, _) in enumerate(sides)]

    for j in range(3):
        arrived(pk.at[j], pack_sem.at[j])
        local.append(pltpu.make_async_copy(pk.at[j], q_ref.at[here_q[j]], own_sem.at[j]))
    last = len(order) - 1
    for k in range(last + 1):
        rs_stage(k, 0)
        if k == 0:
            for cp in own[:3] + local:
                cp.start()
        if k == 2:
            for cp in own[3:]:
                cp.start()
            forward(1)
        if k == 5:
            forward(2)
    for k in range(3):
        rs_stage(k, 1)
    finish(0)
    for cp in spread:
        cp.start()
    for k in range(3, last + 1):
        rs_stage(k, 1)
        if k == 4:
            forward(3)
        if k == last - 1:
            @pl.when(w.c == 0)
            def _():
                for j, (rel, _) in enumerate(sides):
                    arrived(xa_ref.at[rel, :, col[j]], x_r.at[rel, j])
                    relay[j].start()
    forward(4)
    finish(1)

    for cp in own[:1] + own[3:]:
        cp.wait()
    for cp in own[1:3]:
        cp.wait_send()
    local[0].wait()
    for cp in spread:
        cp.wait_send()
    for k in range(len(order)):
        dest = w.chip(order[k])
        arrived(peer.at[dest], peer_s.at[k])
    for i in range(2):
        for dist in range(1, far + 1):
            for h in ((i,) if dist == far else (0, 1)):
                for q in range(2):
                    arrived(part(sb.at[i, dist - 1, h], q), rs_s.at[i, dist - 1, h, q])

    @pl.when(w.c == 1)
    def _():
        for i, dz in enumerate(dirs):
            for h in range(1, far + 1):
                ref = pair(-dz * h) if h < far else single(-dz * h, i)
                if h > 1:
                    arrived(ref, push_s.at[i, h])
                if h < far:
                    arrived(pair(-dz * h) if h < far - 1 else single(-dz * h, i), f_s.at[i, h + 1])

    @pl.when(w.c == 0)
    def _():
        arrived(q_ref.at[pl.ds(0, n_fsdp - 6)], push_r)
        for j in (1, 2):
            local[j].wait()
            own[j].wait_recv()
        arrived(xa_ref.at[0, :, col[1]], x_r.at[0, 0])
        arrived(xb_ref.at[:, col[1]], x_r.at[0, 1])
        arrived(xa_ref.at[2, :, col[1]], x_r.at[2, 1])
        arrived(xa_ref.at[1, :, col[0]], x_r.at[1, 0])
        for j in range(2):
            arrived(xa_ref.at[3, :, col[j]], x_r.at[3, j])
            relay[j].wait_send()
    for h in range(2):
        arrived(xo.at[h], home_sem.at[h])


def embed(side, pc, rows, pq, n0, n1, pe, pd, f0, f1):
    seq, width = rows.shape[2], rows.shape[3]
    nz = pc.n_fsdp // 2
    far = nz // 2
    hbm = pl.BlockSpec(memory_space=pl.ANY)
    dma = pltpu.SemaphoreType.DMA
    return pl.pallas_call(
        functools.partial(embed_kernel, side, pc),
        out_shape=(
            jax.ShapeDtypeStruct((4, seq, width), BF16),
            jax.ShapeDtypeStruct((seq, width), BF16),
            jax.ShapeDtypeStruct((pc.n_fsdp, pc.rows, pc.qkv), BF16),
            jax.ShapeDtypeStruct(pe.shape, BF16),
            jax.ShapeDtypeStruct(pd.shape, BF16),
            jax.ShapeDtypeStruct((2,) + f0.shape, BF16)),
        in_specs=[hbm] * 8,
        out_specs=(hbm,) * 6,
        scratch_shapes=[
            pltpu.VMEM((nz, 2, seq, width // 2), BF16),
            pltpu.VMEM((nz, 2, seq, width // 2), BF16),
            pltpu.VMEM((2, far, 2, seq, width // 2), BF16),
            pltpu.VMEM((2, far, 2, seq, width // 2), BF16),
            pltpu.VMEM((3, pc.rows, pc.qkv), BF16),
            pltpu.VMEM((2, seq, width // 2), BF16),
            dma((nz,)), dma((3,)), dma((3,)), dma((7,)), dma((7,)),
            dma((2, far + 1)), dma((2, far + 1)), dma((2, far + 1)), dma,
            dma((nz,)), dma((nz,)),
            dma((2, far, 2, 2)), dma((2, far, 2, 2)),
            dma((2,)), dma((4,)), dma((4, 2)),
        ],
        compiler_params=pltpu.CompilerParams(collective_id=1, has_side_effects=True, vmem_limit_bytes=67043328),
        name='embed',
    )(rows, pq, n0, n1, pe, pd, f0, f1)


def layer_kernel(side, pc, head_dim, x_ref, xb_ref, q_ref, pe_ref, pd_ref, f0_ref, f1_ref, te_ref, td_ref, tf_ref, g1_ref, g2_ref, cos_ref, sin_ref, out_ref, k_ref, v_ref, w_ref,
                 xa, ca, xm, wg, wd, mm, pp, r1, r2, qf, kvb,
                 lsem, xs_s, xs_r, cs_s, cs_r, ms_s, ms_r, kv_s, kv_r, p1_s, p1_r, p2_s, p2_r, o_s, o_l, o_r,
                 zs, zr, ps, wch):
    h2 = ca
    n_fsdp = pc.n_fsdp
    w = Where(side, n_fsdp)
    far = w.nz // 2
    seq, width = xa.shape[2], xa.shape[3]
    rows_b = 2 * seq
    half = pc.dn_w // 2
    n_chunk = len(pc.chunks)
    last_gu = 5
    greet([w.partner(), w.along_z(1, w.c), w.along_z(-1, w.c)] + [w.square(rel, core) for rel in (1, 2, 3) for core in (0, 1)])
    dirs = (1, -1)

    def slim(t):
        off, cw = pc.chunks[t]
        return pl.ds(off - (pc.qkv if t < pc.early else pc.dn0), cw)

    def own_pieces(t):
        refs = (pe_ref, te_ref) if t < pc.early else (pd_ref, td_ref)
        return [ref.at[:, slim(t)] for ref in refs]

    def near_pieces(t, i):
        return [(f0_ref, f1_ref)[i].at[:, slim(t)], tf_ref.at[i, :, slim(t)]]

    def stream():
        def cols(t):
            off, cw = pc.chunks[t]
            return pl.ds(off - pc.qkv, cw)

        def pair(t, dz):
            return w_ref.at[pl.ds(2 * w.chip(dz), 2), :, cols(t)]

        def single(t, dz, i):
            return w_ref.at[pl.ds(2 * w.chip(dz) + i, 1), :, cols(t)]

        def piece(t, h, i):
            dz = dirs[i]
            return pair(t, -dz * h) if h < far else single(t, -dz * h, i)

        sent = []

        def hop(t, h):
            if t < 1 or t >= n_chunk or (h == 0 and t < pc.early):
                return
            ready = h == 1 and t < pc.early
            for i in range(2):
                dz = dirs[i]
                if h > 0 and not ready:
                    arrived(piece(t, h, i), zr.at[t, i, h])
                if h == far:
                    continue
                ref = pair(t, -dz * h) if h < far - 1 else single(t, -dz * h, i)
                sems = (zs.at[t, i, h], zr.at[t, i, h + 1], w.along_z(dz, 1))
                if h == 0 or ready:
                    pieces = near_pieces(t, i) if ready else own_pieces(t)
                    for src, core in zip(pieces, (1, 0)):
                        remote(src, w_ref.at[2 * w.chip(-dz * h) + core, :, cols(t)], *sems).start()
                else:
                    remote(ref, ref, *sems).start()
                sent.append((ref, zs.at[t, i, h]))
            if h > 0 and not ready:
                for i in range(2):
                    ref = piece(t, h, i)
                    remote(ref, ref, ps.at[t, i, h], wch.at[t], w.partner()).start()
                    sent.append((ref, ps.at[t, i, h]))

        for s in range(2, n_chunk + far):
            for h in range(far + 1):
                hop(s - h, h)
        for ref, sem in sent:
            arrived(ref, sem)
        kvw = 2 * (kvb.shape[2] // 4)
        for rel in range(4):
            arrived(k_ref.at[:, pl.ds(0, kvw)], kv_r.at[rel, 0])
            arrived(v_ref.at[:, pl.ds(0, kvw)], kv_r.at[rel, 1])
        for n in range(4):
            arrived(out_ref.at[:, pl.ds(n * pc.dn_w, pc.dn_w)], o_r.at[n])

    def compute():
        y, x = w.square(1, 0), w.square(2, 0)
        q4, kv4 = pc.q4, pc.kv4
        cols = {q: aligned((w.me ^ q) * pc.w4, pc.w4, LANES) for q in range(4)}
        sent = []

        def go(cp):
            cp.start()
            sent.append(cp)

        def load(t, dst, sem):
            off, cw = pc.chunks[t]
            c = pl.ds(off - pc.qkv, cw)
            near = t < pc.early
            arrived(w_ref.at[pl.ds(0, n_fsdp - (6 if near else 2)), :, c], wch.at[t])
            for dz in range(-1, w.nz - 1):
                two = pl.ds(2 * w.chip(dz), 2)
                if dz == 0 or (near and dz in (1, -1)):
                    pieces = own_pieces(t) if dz == 0 else near_pieces(t, 0 if dz == -1 else 1)
                    for core, src in enumerate(pieces):
                        pltpu.make_async_copy(src, dst.at[2 * w.chip(dz) + core], sem).start()
                else:
                    pltpu.make_async_copy(w_ref.at[two, :, c], dst.at[two], sem).start()

        own = [pltpu.make_async_copy(x_ref, xa.at[:, 0], lsem.at[0]),
               pltpu.make_async_copy(xb_ref, xa.at[0, 1], lsem.at[2]),
               pltpu.make_async_copy(q_ref, wg.at[:, :, pl.ds(0, pc.qkv)], lsem.at[1])]
        for cp in own:
            cp.start()
        bits = [pl.ds(j * (seq // 2), seq // 2) for j in range(2)]
        for j, (rel, dev, q) in enumerate(((2, x, 0), (1, y, 1), (2, x, 1), (1, y, 0))):
            go(remote(xb_ref.at[bits[q]], xa.at[rel, 1, bits[q]], xs_s.at[j], xs_r.at[rel, q], dev))
        for cp in own:
            cp.wait()

        def norm_into(dst, slot, load_rows, gain_ref):
            def one(i, carry):
                rows = aligned(i * 16, 16, 16)
                val = load_rows(rows, i).astype(F32)
                inv = lax.rsqrt(jnp.mean(val * val, axis=-1, keepdims=True) + NORM_EPS)
                dst[slot, rows, :] = (val * inv * gain_ref[...]).astype(BF16)
                return carry
            lax.fori_loop(0, rows_b // 16, one, 0)

        per = seq // 16
        lane = lax.broadcasted_iota(jnp.int32, (seq, LANES), 1)
        low_head = (lane % head_dim) < head_dim // 2
        first_head = lane < head_dim
        n_pair = q4 // LANES
        pair_per_kv = n_pair // 2

        def rope(t):
            swapped = jnp.where(low_head, pltpu.roll(t, LANES - head_dim // 2, 1), pltpu.roll(t, head_dim // 2, 1))
            return t * cos_ref[...] + swapped * sin_ref[...]

        def attend(base, h):
            norm_into(mm, 0, lambda rows, i: xa[base + 2 * (i // per), h, aligned((i % per) * 16, 16, 16), :], g1_ref)

            def proj(nt, carry):
                c = aligned(nt * 256, 256, LANES)
                qf[:, c] = jnp.dot(mm[0], wg[:, :, c].reshape(width, 256), preferred_element_type=F32)
                return carry
            lax.fori_loop(0, pc.qkv // 256, proj, 0)

            def one_seq(u, carry):
                slot = base + 2 * u
                rows = aligned(u * seq, seq, seq)
                place = pl.ds(h * seq, seq)
                k_f = rope(qf[rows, pl.ds(q4, LANES)])
                v_f = qf[rows, pl.ds(q4 + kv4, LANES)]
                kvb[slot, place, pl.ds(0, LANES)] = k_f.astype(BF16)
                kvb[slot, place, pl.ds(LANES, LANES)] = v_f.astype(BF16)
                k_r, v_r = pltpu.roll(k_f, head_dim, 1), pltpu.roll(v_f, head_dim, 1)
                zero = jnp.zeros_like(k_f)
                row = lax.broadcasted_iota(jnp.int32, (pair_per_kv * seq, seq), 0) % seq
                causal = row >= lax.broadcasted_iota(jnp.int32, (pair_per_kv * seq, seq), 1)
                for g in range(2):
                    k_lo, k_hi = (k_f, k_r) if g == 0 else (k_r, k_f)
                    v_lo, v_hi = (v_f, v_r) if g == 0 else (v_r, v_f)
                    kk = jnp.concatenate([jnp.where(first_head, k_lo, zero), jnp.where(first_head, zero, k_hi)], axis=0).astype(BF16)
                    vv = jnp.concatenate([jnp.where(first_head, v_lo, zero), jnp.where(first_head, zero, v_hi)], axis=0).astype(BF16)
                    qs = jnp.concatenate([rope(qf[rows, pl.ds((g * pair_per_kv + p) * LANES, LANES)]).astype(BF16) for p in range(pair_per_kv)], axis=0)
                    sc = lax.dot_general(qs, kk, (((1,), (1,)), ((), ())), preferred_element_type=F32) * (head_dim ** -0.5)
                    probs = []
                    for e in range(2):
                        part = jnp.where(causal, sc[:, e * seq:(e + 1) * seq], -jnp.inf)
                        part = jnp.exp(part - jnp.max(part, axis=-1, keepdims=True))
                        probs.append((part / jnp.sum(part, axis=-1, keepdims=True)).astype(BF16))
                    ctx = jnp.dot(jnp.concatenate(probs, axis=1), vv, preferred_element_type=F32).astype(BF16)
                    for p in range(pair_per_kv):
                        lanes = aligned(w.me * pc.w4 + (g * pair_per_kv + p) * LANES, LANES, LANES)
                        ca[slot, place, lanes] = ctx[p * seq:(p + 1) * seq]
                return carry
            lax.fori_loop(0, 2, one_seq, 0)

        whole = pl.ds(0, rows_b)

        def spread(buf, slot, ss, rs, rows=whole, idx=()):
            mine = buf.at[slot, rows, cols[0]]
            go(remote(mine, buf.at[slot ^ 2, rows, cols[0]], ss.at[(slot,) + idx + (1,)], rs.at[(slot ^ 2,) + idx + (1,)], x))
            go(remote(mine, buf.at[slot ^ 1, rows, cols[0]], ss.at[(slot,) + idx + (0,)], rs.at[(slot ^ 1,) + idx + (0,)], y))

        def take(buf, slot, q, rs, rows=whole, idx=()):
            arrived(buf.at[slot, rows, cols[q]], rs.at[(slot,) + idx + (q - 1 if q < 3 else 2,)])

        def relay(buf, slot, q, ss, rs, rows=whole, idx=()):
            take(buf, slot, q, rs, rows, idx)
            ref = buf.at[slot, rows, cols[q]]
            to, dev = (slot ^ 1, y) if q == 2 else (slot ^ 2, x)
            go(remote(ref, buf.at[to, rows, cols[q]], ss.at[(to,) + idx + (2,)], rs.at[(to,) + idx + (2,)], dev))

        def send_kv(slot):
            mine = aligned(w.me * kv4, kv4, LANES)
            for core in range(2):
                for j, dst in enumerate((k_ref, v_ref)):
                    src = kvb.at[slot, pl.ds(core * seq, seq), pl.ds(j * kv4, kv4)]
                    if slot == 0 and core == 0:
                        cp = pltpu.make_async_copy(src, dst.at[:, mine], kv_s.at[slot, core, j])
                        cp.start()
                        local_kv.append(cp)
                    else:
                        go(remote(src, dst.at[:, mine], kv_s.at[slot, core, j], kv_r.at[slot, j], w.square(slot, core)))
        local_kv = []

        def here(slot, q):
            arrived(xa.at[slot, 1, bits[q]], xs_r.at[slot, q])

        seqs = [pl.ds(h * seq, seq) for h in range(2)]

        def send_ctx(base, h):
            for slot in (base, base + 2):
                spread(ca, slot, cs_s, cs_r, seqs[h], (h,))

        def relay_ctx(q, h):
            for slot in ((2, 0) if q == 2 else (0, 2)):
                relay(ca, slot, q, cs_s, cs_r, seqs[h], (h,))

        attend(0, 0)
        send_ctx(0, 0)
        here(2, 0)
        go(remote(xa.at[2, 1, bits[0]], xa.at[3, 1, bits[0]], xs_s.at[4], xs_r.at[3, 0], y))
        here(1, 1)
        go(remote(xa.at[1, 1, bits[1]], xa.at[3, 1, bits[1]], xs_s.at[5], xs_r.at[3, 1], x))
        attend(1, 0)
        send_ctx(1, 0)
        relay_ctx(2, 0)
        here(2, 1)
        attend(0, 1)
        send_ctx(0, 1)
        relay_ctx(1, 0)
        for slot, q in ((1, 0), (3, 0), (3, 1)):
            here(slot, q)
        attend(1, 1)
        send_ctx(1, 1)
        relay_ctx(2, 1)
        relay_ctx(1, 1)
        load(1, wd, lsem.at[0])
        for slot in range(4):
            send_kv(slot)
        arrived(wd, lsem.at[0])
        n_ctx = len(sent)

        def mid(slot):
            for q in (1, 2, 3):
                if q == 3 or slot in (1, 3):
                    for h in range(2):
                        take(ca, slot, q, cs_r, seqs[h], (h,))

            def one(nt, carry):
                c = aligned(nt * 256, 256, LANES)
                o = aligned(w.me * pc.w4 + nt * 256, 256, LANES)
                got = jnp.dot(ca[slot], wd[:, :, c].reshape(width, 256), preferred_element_type=F32)
                res = xa[slot, :, :, o].reshape(rows_b, 256).astype(F32)
                xm[slot, :, o] = (res + got).astype(BF16)
                return carry
            lax.fori_loop(0, pc.w4 // 256, one, 0)
            spread(xm, slot, ms_s, ms_r)

        mid(3)
        mid(1)
        mid(2)
        relay(xm, 1, 2, ms_s, ms_r)
        mid(0)
        relay(xm, 3, 2, ms_s, ms_r)
        relay(xm, 3, 1, ms_s, ms_r)
        relay(xm, 1, 1, ms_s, ms_r)
        for cp in sent[:n_ctx]:
            cp.wait_send()
        del sent[:n_ctx]
        for slot in (0, 2, 1, 3):
            for q in (1, 2, 3):
                if q == 3 or slot in (0, 2):
                    take(xm, slot, q, ms_r)
            norm_into(h2, slot, lambda rows, i, slot=slot: xm[slot, rows, :], g2_ref)

        gate_w = pc.gu_w // 2
        for b in range(4):
            load(2 + b, wg, lsem.at[b % 2])
            arrived(wg, lsem.at[b % 2])

            def one(j, carry):
                s, nt = j // (gate_w // 256), j % (gate_w // 256)
                act = h2[pl.ds(2 * s, 2)].reshape(2 * rows_b, width)
                gate = jnp.dot(act, wg[:, :, aligned(nt * 256, 256, LANES)].reshape(width, 256), preferred_element_type=F32)
                up = jnp.dot(act, wg[:, :, aligned(gate_w + nt * 256, 256, LANES)].reshape(width, 256), preferred_element_type=F32)
                val = (jax.nn.silu(gate) * up).astype(BF16)
                mm[pl.ds(2 * s, 2), :, aligned(b * gate_w + nt * 256, 256, LANES)] = val.reshape(2, rows_b, 256)
                return carry
            lax.fori_loop(0, 2 * (gate_w // 256), one, 0)

        h0, h1 = pl.ds(0, half), pl.ds(half, half)
        first_sends, home = {}, []

        def phase1(n):
            load(last_gu + 1 + n, wd, lsem.at[n % 2])
            for old in first_sends.get(n - 2, ()):
                old.wait_send()
            arrived(wd, lsem.at[n % 2])
            par = n % 2

            def one(j, carry):
                s, nt = j // (pc.dn_w // 256), j % (pc.dn_w // 256)
                c = aligned(nt * 256, 256, LANES)
                act = mm[pl.ds(2 * s, 2)].reshape(2 * rows_b, mm.shape[2])
                got = jnp.dot(act, wd[:, :, c].reshape(mm.shape[2], 256), preferred_element_type=F32)
                pp[par, pl.ds(2 * s, 2), :, c] = got.reshape(2, rows_b, 256)
                return carry
            lax.fori_loop(0, 2 * (pc.dn_w // 256), one, 0)
            first_sends[n] = []
            for path, dev, cc, rels in ((0, x, h0, (2, 3)), (1, y, h1, (1, 3))):
                for j, rel in enumerate(rels):
                    cp = remote(pp.at[par, rel, :, cc], r1.at[n, path, j], p1_s.at[n, path, j], p1_r.at[n, path, j], dev)
                    cp.start()
                    first_sends[n].append(cp)

        def phase2(n):
            par = n % 2
            for path, dev, cc, rel in ((0, y, h0, 1), (1, x, h1, 2)):
                arrived(r1.at[n, path, 1], p1_r.at[n, path, 1])
                r1[n, path, 1] = pp[par, rel, :, cc] + r1[n, path, 1]
                go(remote(r1.at[n, path, 1], r2.at[n, path], p2_s.at[n, path], p2_r.at[n, path], dev))
            for path, cc in ((0, h0), (1, h1)):
                arrived(r1.at[n, path, 0], p1_r.at[n, path, 0])
                r1[n, path, 0] = pp[par, 0, :, cc] + r1[n, path, 0]

        def phase3(n):
            for path in range(2):
                arrived(r2.at[n, path], p2_r.at[n, path])
                c = pl.ds(n * pc.dn_w + path * half, half)
                total = xm[0, :, c].astype(F32) + (r1[n, path, 0] + r2[n, path])
                xm[0, :, c] = total.astype(BF16)
            c = pl.ds(n * pc.dn_w, pc.dn_w)
            go(remote(xm.at[0, pl.ds(seq, seq), c], out_ref.at[:, c], o_s.at[n], o_r.at[n], w.partner()))
            cp = pltpu.make_async_copy(xm.at[0, pl.ds(0, seq), c], out_ref.at[:, c], o_l.at[n])
            cp.start()
            home.append(cp)

        for cp in sent:
            cp.wait_send()
        sent.clear()
        for n in range(4):
            phase1(n)
            if n >= 1:
                phase2(n - 1)
            if n >= 2:
                phase3(n - 2)
        phase2(3)
        phase3(2)
        phase3(3)

        for cp in sent:
            cp.wait_send()
        for n in (2, 3):
            for cp in first_sends[n]:
                cp.wait_send()
        for cp in local_kv + home:
            cp.wait()
        for rel in (1, 2, 3):
            arrived(k_ref.at[:, pl.ds(0, kv4)], kv_r.at[rel, 0])
            arrived(v_ref.at[:, pl.ds(0, kv4)], kv_r.at[rel, 1])

    pl.when(w.c == 1)(stream)
    pl.when(w.c == 0)(compute)


def layer(side, pc, head_dim, x, xb, q_all, near, g1, g2, cos_tab, sin_tab):
    _, seq, width = x.shape
    rows_b = 2 * seq
    kv_width = 4 * pc.kv4
    n_chunk = len(pc.chunks)
    far = pc.n_fsdp // 4
    ff4 = pc.f4 * pc.n_fsdp
    half = pc.dn_w // 2
    hbm = pl.BlockSpec(memory_space=pl.ANY)
    vmem = pl.BlockSpec(memory_space=pltpu.VMEM)
    dma = pltpu.SemaphoreType.DMA
    return pl.pallas_call(
        functools.partial(layer_kernel, side, pc, head_dim),
        out_shape=(
            jax.ShapeDtypeStruct((seq, width), BF16),
            jax.ShapeDtypeStruct((seq, kv_width), BF16),
            jax.ShapeDtypeStruct((seq, kv_width), BF16),
            jax.ShapeDtypeStruct((pc.n_fsdp, pc.rows, pc.late), BF16)),
        in_specs=[hbm] * (3 + len(near)) + [vmem, vmem, vmem, vmem],
        out_specs=(hbm, hbm, hbm, hbm),
        scratch_shapes=[
            pltpu.VMEM((4, 2, seq, width), BF16),
            pltpu.VMEM((4, rows_b, width), BF16),
            pltpu.VMEM((4, rows_b, width), BF16),
            pltpu.VMEM((pc.n_fsdp, pc.rows, pc.gu_w), BF16),
            pltpu.VMEM((pc.n_fsdp, pc.rows, pc.dn_w), BF16),
            pltpu.VMEM((4, rows_b, max(ff4, width)), BF16),
            pltpu.VMEM((2, 4, rows_b, pc.dn_w), F32),
            pltpu.VMEM((4, 2, 2, rows_b, half), F32),
            pltpu.VMEM((4, 2, rows_b, half), F32),
            pltpu.VMEM((rows_b, pc.qkv), F32),
            pltpu.VMEM((4, rows_b, 2 * pc.kv4), BF16),
            dma((3,)),
            dma((6,)), dma((4, 2)),
            dma((4, 2, 3)), dma((4, 2, 3)),
            dma((4, 3)), dma((4, 3)),
            dma((4, 2, 2)), dma((4, 2)),
            dma((4, 2, 2)), dma((4, 2, 2)),
            dma((4, 2)), dma((4, 2)),
            dma((4,)), dma((4,)), dma((4,)),
            dma((n_chunk, 2, far + 1)), dma((n_chunk, 2, far + 1)), dma((n_chunk, 2, far + 1)), dma((n_chunk,)),
        ],
        compiler_params=pltpu.CompilerParams(collective_id=2, has_side_effects=True, vmem_limit_bytes=67043328),
        name='layer',
    )(x, xb, q_all, *near, g1, g2, cos_tab, sin_tab)


def solution(mesh):
    batch_axes = ('dp', 'fsdp')
    row_spec = P('fsdp', None)
    n_dp = mesh.shape['dp']
    n_fsdp = mesh.shape['fsdp']
    side = math.isqrt(n_dp)

    def device_step(tokens, embed_table, norm_attn, w_qkv, w_out, norm_mlp, w_gate_up, w_down, rope_scale):
        seq = tokens.shape[1]
        shard_rows, width = embed_table.shape
        head_dim = 2 * rope_scale.shape[0]
        rows = w_out.shape[0]
        q_width = rows * n_fsdp
        kv_width = (w_qkv.shape[1] - q_width) // 2
        pc = Pieces(rows, q_width // 4, kv_width // 4, width // 4, w_down.shape[0] // 4, n_fsdp, width)

        gains = jnp.stack([norm_attn, norm_mlp]).astype(F32)
        ids, gains, pq, pe, pd = gather_ids(side, pc, tokens, gains, w_qkv, w_out, w_gate_up, w_down)
        def first_hop(piece, dz):
            return lax.ppermute(piece, 'fsdp', [(i, (i + 2 * dz) % n_fsdp) for i in range(n_fsdp)])

        n0, n1 = first_hop(pq, 1), first_hop(pq, -1)
        f0, f1 = first_hop(pe, 1), first_hop(pe, -1)
        ids = ids.reshape(-1) - lax.axis_index('fsdp') * shard_rows
        owned = (ids >= 0) & (ids < shard_rows)
        table_rows = gather_table(ids, owned, embed_table)
        g1 = gains[:, 0].reshape(1, width)
        g2 = gains[:, 1].reshape(1, width)

        freq_expo = jnp.arange(head_dim // 2, dtype=F32) * (2.0 / head_dim)
        inv_freq = 1.0 / (rope_scale * jnp.power(ROPE_THETA, freq_expo))
        angles = jnp.arange(seq, dtype=F32)[:, None] * inv_freq[None, :]
        cos_tab, sin_tab = jnp.cos(angles), jnp.sin(angles)
        reps = LANES // head_dim
        cos_tab = jnp.concatenate([cos_tab, cos_tab] * reps, axis=1)
        sin_tab = jnp.concatenate([-sin_tab, sin_tab] * reps, axis=1)

        table_rows = table_rows.reshape(n_fsdp // 2, 2, seq, width)
        x, xb, q_all, te, td, tf = embed(side, pc, table_rows, pq, n0, n1, pe, pd, f0, f1)
        out, k, v, _ = layer(side, pc, head_dim, x, xb, q_all, (pe, pd, f0, f1, te, td, tf), g1, g2, cos_tab, sin_tab)
        heads = (1, seq, kv_width // head_dim, head_dim)
        return out[None], k.reshape(heads), v.reshape(heads)

    return jax.shard_map(
        device_step,
        mesh=mesh,
        in_specs=(P(batch_axes, None), row_spec, P('fsdp'), row_spec, row_spec, P('fsdp'), row_spec, row_spec, P(None)),
        out_specs=(P(batch_axes, None, None), P(batch_axes, None, None, None), P(batch_axes, None, None, None)),
        check_vma=False,
    )
```

profile of v0, /device:TPU:21, one launch (start us, length us, event | category | flops | bytes accessed | tf_op | source)
XLA Modules:
  0.0 275.3 jit_solution(3595052123949924190)
XLA Ops:
  0.6 1.2 maximum_convert_fusion.gain_ref
  1.9 15.6 %ids.1 = (s32[16,1,128]{2,1,0:T(1,128)}, f32[16,2,128]{2,1,0:T(2,128)}, bf16[128,768]{1,0:T(8,128)(2,1)}, bf16[128,4608]{1,0:T(8,128)(2,1)}, bf16[128,2048]{1,0:T(8,128)(2,1)}) custom-call(s32[1,128]{1,0:T(1,128)} %tok_ref.1, f32[2,128]{1,0:T(2,128)} %maximum_convert_fusion.gain_ref, bf16[128,3072]{1,0:T(8,128)(2,1)} %w_qkv.1, bf16[128,2048]{1,0:T(8,128)(2,1)} %w_out.1, ...), custom_call_target="tpu_custom_call" | custom-call | tf_op jit(solution)/shard_map/ids/pallas_call | solution.py:144
  17.5 2.2 collective-permute-start.1
  19.7 0.0 collective-permute-start
  19.7 2.7 collective-permute-start.3
  22.4 0.0 collective-permute-start.2
  22.4 0.7 fusion.16
  23.1 0.7 broadcast_subtract_fusion
  23.8 0.4 copy.14
  24.2 0.6 fusion.2.tgt_ref
  24.8 0.0 copy-start.1
  24.8 0.0 copy-start
  24.8 30.5 %rows.1 = bf16[2048,2048]{1,0:T(8,128)(2,1)} custom-call(s32[2048]{0:T(1024)S(1)} %fusion.11.gid_ref, s32[2048,1]{1,0:T(8,128)S(1)} %fusion.2.tgt_ref, bf16[1002,8,2048]{2,1,0:T(8,128)(2,1)} %bitcast.24), custom_call_target="tpu_custom_call" | custom-call | flops 80000000000 | bytes 75497472 | tf_op jit(solution)/shard_map/rows/pallas_call | solution.py:192
  55.4 0.0 copy-done.1
  55.4 0.0 copy-done
  55.4 0.6 slice_bitcast_fusion
  56.0 0.3 fusion.9
  56.3 0.8 pad_maximum_fusion
  57.1 0.0 collective-permute-done.1.n1_ref
  57.1 0.0 collective-permute-done.n0_ref
  57.1 0.0 collective-permute-done.3.f1_ref
  57.1 0.0 collective-permute-done.2.f0_ref
  57.1 68.2 %embed.1 = (bf16[4,128,2048]{2,1,0:T(8,128)(2,1)}, bf16[128,2048]{1,0:T(8,128)(2,1)}, bf16[16,128,768]{2,1,0:T(8,128)(2,1)}, bf16[128,4608]{1,0:T(8,128)(2,1)}, ...) custom-call(bf16[8,2,128,2048]{3,2,1,0:T(8,128)(2,1)} %bitcast.16, bf16[128,768]{1,0:T(8,128)(2,1)} %get-tuple-element.18.pq_ref, ...), custom_call_target="tpu_custom_call" | custom-call | tf_op jit(solution)/shard_map/embed/pallas_call | solution.py:412
  125.4 144.7 %layer.1 = (bf16[128,2048]{1,0:T(8,128)(2,1)}, bf16[128,512]{1,0:T(8,128)(2,1)}, bf16[128,512]{1,0:T(8,128)(2,1)}, bf16[16,128,6656]{2,1,0:T(8,128)(2,1)}) custom-call(bf16[4,128,2048]{2,1,0:T(8,128)(2,1)} %get-tuple-element.21.x_ref, bf16[128,2048]{1,0:T(8,128)(2,1)} %get-tuple-element.22.xb_ref, bf16[16,128,768]{2,1,0:T(8,128)(2,1)} %get-tuple-element.23.q_ref, ...), custom_call_target="tpu_custom_call" | custom-call | tf_op jit(solution)/shard_map/layer/pallas_call | solution.py:818
  270.1 1.7 copy.19
  271.8 1.7 copy.20
  273.4 1.9 copy.22
  (2 shorter events, 0.0 us)
Async XLA Ops:
  17.5 39.6 %collective-permute-start.1 = (bf16[128,768]{1,0:T(8,128)(2,1)}, bf16[128,768]{1,0:T(8,128)(2,1)}, u32[]{:S(2)}, u32[]{:S(2)}) collective-permute-start(bf16[128,768]{1,0:T(8,128)(2,1)} %get-tuple-element.18.pq_ref), channel_id=1, source_target_pairs={{0,14},{1,15},{2,0},{3,1},{4,2},{5,3},{6,4},{7,5},{8,6},{9,7},{10,... | collective-permute-start | bytes 589832 | tf_op jit(solution)/shard_map/ppermute | solution.py:873
  19.7 37.4 %collective-permute-start = (bf16[128,768]{1,0:T(8,128)(2,1)}, bf16[128,768]{1,0:T(8,128)(2,1)}, u32[]{:S(2)}, u32[]{:S(2)}) collective-permute-start(bf16[128,768]{1,0:T(8,128)(2,1)} %get-tuple-element.18.pq_ref), channel_id=1, source_target_pairs={{0,2},{1,3},{2,4},{3,5},{4,6},{5,7},{6,8},{7,9},{8,10},{9,11},{10,... | collective-permute-start | bytes 589832 | tf_op jit(solution)/shard_map/ppermute | solution.py:873
  19.7 37.4 %collective-permute-start.3 = (bf16[128,4608]{1,0:T(8,128)(2,1)}, bf16[128,4608]{1,0:T(8,128)(2,1)}, u32[]{:S(2)}, u32[]{:S(2)}) collective-permute-start(bf16[128,4608]{1,0:T(8,128)(2,1)} %get-tuple-element.19.pe_ref), channel_id=1, source_target_pairs={{0,14},{1,15},{2,0},{3,1},{4,2},{5,3},{6,4},{7,5},{8,6},{9,7},{10,... | collective-permute-start | bytes 3538952 | tf_op jit(solution)/shard_map/ppermute | solution.py:873
  22.4 34.8 %collective-permute-start.2 = (bf16[128,4608]{1,0:T(8,128)(2,1)}, bf16[128,4608]{1,0:T(8,128)(2,1)}, u32[]{:S(2)}, u32[]{:S(2)}) collective-permute-start(bf16[128,4608]{1,0:T(8,128)(2,1)} %get-tuple-element.19.pe_ref), channel_id=1, source_target_pairs={{0,2},{1,3},{2,4},{3,5},{4,6},{5,7},{6,8},{7,9},{8,10},{9,11},{10,... | collective-permute-start | bytes 3538952 | tf_op jit(solution)/shard_map/ppermute | solution.py:873
  24.8 30.6 %copy-start.1 = (f32[32]{0:T(128)S(1)}, f32[32]{0:T(128)}, u32[]{:S(2)}) copy-start(f32[32]{0:T(128)} %param.17) | copy-start | bytes 388
  24.8 30.6 %copy-start = (f32[16,2,128]{2,1,0:T(2,128)S(1)}, f32[16,2,128]{2,1,0:T(2,128)}, u32[]{:S(2)}) copy-start(f32[16,2,128]{2,1,0:T(2,128)} %get-tuple-element.27) | copy-start | bytes 49156
where the time goes:
time: 278 us; the launch traced here: 275 us
  Pallas kernels  259 us (93%)
  local copies, waits for them, and re-layouts  6.2 us (2%)
  starting transfers between devices  4.87 us (2%)
  other arithmetic  4.4 us (2%)
    pallas_call x1, Pallas kernels, layer(): pl.pallas_call(functools.partial(layer_kernel, side, pc, head_dim), out_s...  145 us
    pallas_call x1, Pallas kernels, embed(): pl.pallas_call(functools.partial(embed_kernel, side, pc), out_shape=(jax....  68.2 us
    pallas_call x1, Pallas kernels, gather_table(): pl.pallas_call(functools.partial(gather_kernel, n_tok), out_shape=jax.Sha...  30.5 us
    pallas_call x1, Pallas kernels, gather_ids(): pl.pallas_call(functools.partial(ids_kernel, side, pc), out_shape=(jax.Sh...  15.6 us
  transfers between devices with their start and end apart: 4, of which 0 were waited for; matrix products, arithmetic and copies ran while one was open for 2% of the time, Pallas kernels for 11%

commit v1 on v0

--- a/solution.py
+++ b/solution.py
@@ -64,7 +64,7 @@
     pltpu.make_async_copy(ref, ref, sem).wait()
 
 
-def ids_kernel(side, pc, tok_ref, gain_ref, w_qkv, w_out, w_gu, w_dn, ids_ref, gains_ref, pq_ref, pe_ref, pd_ref,
+def ids_kernel(side, pc, tok_ref, gain_ref, w_qkv, w_out, w_gu, w_dn, ids_ref, gains_ref, pe_ref, pd_ref,
                pk, lsem, ssem, rsem, pack_sem, store_sem):
     n_fsdp = pc.n_fsdp
     w = Where(side, n_fsdp)
@@ -84,7 +84,7 @@
     arrived(pk, pack_sem)
     lo = 0
     stores = []
-    for j, ref in enumerate((pq_ref, pe_ref, pd_ref)):
+    for j, ref in enumerate((pe_ref, pd_ref)):
         stores.append(pltpu.make_async_copy(pk.at[:, pl.ds(lo, ref.shape[1])], ref, store_sem.at[j]))
         stores[-1].start()
         lo += ref.shape[1]
@@ -146,12 +146,11 @@
         out_shape=(
             jax.ShapeDtypeStruct((n_fsdp,) + tokens.shape, tokens.dtype),
             jax.ShapeDtypeStruct((n_fsdp,) + gains.shape, gains.dtype),
-            jax.ShapeDtypeStruct((pc.rows, pc.qkv), BF16),
-            jax.ShapeDtypeStruct((pc.rows, pc.dn0 - pc.qkv), BF16),
+            jax.ShapeDtypeStruct((pc.rows, pc.dn0), BF16),
             jax.ShapeDtypeStruct((pc.rows, pc.width), BF16)),
         in_specs=[vmem, vmem, hbm, hbm, hbm, hbm],
-        out_specs=(vmem, vmem, hbm, hbm, hbm),
-        scratch_shapes=[pltpu.VMEM((pc.rows, pc.total), BF16), dma((2,)), dma((2, n_fsdp)), dma((2, n_fsdp)), dma, dma((3,))],
+        out_specs=(vmem, vmem, hbm, hbm),
+        scratch_shapes=[pltpu.VMEM((pc.rows, pc.total), BF16), dma((2,)), dma((2, n_fsdp)), dma((2, n_fsdp)), dma, dma((2,))],
         compiler_params=pltpu.CompilerParams(collective_id=0, has_side_effects=True),
         name='ids',
     )(tokens, gains, w_qkv, w_out, w_gu, w_dn)
@@ -201,7 +200,7 @@
     )(gid, tgt, table.reshape(n_rows // 8, 8, width))
 
 
-def embed_kernel(side, pc, rows_ref, pq_ref, n0_ref, n1_ref, pe_ref, pd_ref, f0_ref, f1_ref, xa_ref, xb_ref, q_ref, te_ref, td_ref, tf_ref,
+def embed_kernel(side, pc, rows_ref, pe_ref, pd_ref, f0_ref, f1_ref, xa_ref, xb_ref, q_ref, te_ref, td_ref, tf_ref,
                  got, peer, rp, sb, pk, xo,
                  got_sem, pack_sem, own_sem, d2d_s, d2d_r, f_s, f_r, push_s, push_r,
                  peer_s, peer_r, rs_s, rs_r, home_sem, x_s, x_r):
@@ -221,7 +220,8 @@
     for k in range(len(order)):
         dest = w.chip(order[k])
         pltpu.make_async_copy(rows_ref.at[dest, :, :, mine], got.at[dest], got_sem.at[k]).start()
-    for j, src in enumerate((pq_ref, n0_ref, n1_ref)):
+    q_srcs = [ref.at[:, pl.ds(0, pc.qkv)] for ref in (pe_ref, f0_ref, f1_ref)]
+    for j, src in enumerate(q_srcs):
         pltpu.make_async_copy(src, pk.at[j], pack_sem.at[j]).start()
     greet([w.partner()] + [w.along_z(dz, core) for dz in (1, -1) for core in (0, 1)] + [w.square(rel, core) for rel in (1, 2) for core in (0, 1)])
     dirs = (1, -1)
@@ -231,8 +231,9 @@
         remote(rows_ref.at[dest, :, :, other], peer.at[dest], peer_s.at[k], peer_r.at[k], w.partner()).start()
 
     here_q = (2 * w.z + w.c, 2 * w.chip(-1) + w.c, 2 * w.chip(1) + w.c)
-    swaps = [(src, q_ref.at[here_q[j]]) for j, src in enumerate((pq_ref, n0_ref, n1_ref))]
-    swaps += [(pe_ref, te_ref), (pd_ref, td_ref), (f0_ref, tf_ref.at[0]), (f1_ref, tf_ref.at[1])]
+    swaps = [(src, q_ref.at[here_q[j]]) for j, src in enumerate(q_srcs)]
+    rest = pl.ds(pc.qkv, pc.dn0 - pc.qkv)
+    swaps += [(pe_ref.at[:, rest], te_ref), (pd_ref, td_ref), (f0_ref.at[:, rest], tf_ref.at[0]), (f1_ref.at[:, rest], tf_ref.at[1])]
     own = [remote(src, dst, d2d_s.at[j], d2d_r.at[j], w.partner()) for j, (src, dst) in enumerate(swaps)]
 
 
@@ -403,7 +404,7 @@
         arrived(xo.at[h], home_sem.at[h])
 
 
-def embed(side, pc, rows, pq, n0, n1, pe, pd, f0, f1):
+def embed(side, pc, rows, pe, pd, f0, f1):
     seq, width = rows.shape[2], rows.shape[3]
     nz = pc.n_fsdp // 2
     far = nz // 2
@@ -415,10 +416,10 @@
             jax.ShapeDtypeStruct((4, seq, width), BF16),
             jax.ShapeDtypeStruct((seq, width), BF16),
             jax.ShapeDtypeStruct((pc.n_fsdp, pc.rows, pc.qkv), BF16),
-            jax.ShapeDtypeStruct(pe.shape, BF16),
+            jax.ShapeDtypeStruct((pc.rows, pc.dn0 - pc.qkv), BF16),
             jax.ShapeDtypeStruct(pd.shape, BF16),
-            jax.ShapeDtypeStruct((2,) + f0.shape, BF16)),
-        in_specs=[hbm] * 8,
+            jax.ShapeDtypeStruct((2, pc.rows, pc.dn0 - pc.qkv), BF16)),
+        in_specs=[hbm] * 5,
         out_specs=(hbm,) * 6,
         scratch_shapes=[
             pltpu.VMEM((nz, 2, seq, width // 2), BF16),
@@ -435,7 +436,7 @@
         ],
         compiler_params=pltpu.CompilerParams(collective_id=1, has_side_effects=True, vmem_limit_bytes=67043328),
         name='embed',
-    )(rows, pq, n0, n1, pe, pd, f0, f1)
+    )(rows, pe, pd, f0, f1)
 
 
 def layer_kernel(side, pc, head_dim, x_ref, xb_ref, q_ref, pe_ref, pd_ref, f0_ref, f1_ref, te_ref, td_ref, tf_ref, g1_ref, g2_ref, cos_ref, sin_ref, out_ref, k_ref, v_ref, w_ref,
@@ -454,16 +455,16 @@
     greet([w.partner(), w.along_z(1, w.c), w.along_z(-1, w.c)] + [w.square(rel, core) for rel in (1, 2, 3) for core in (0, 1)])
     dirs = (1, -1)
 
-    def slim(t):
+    def slim(t, mine):
         off, cw = pc.chunks[t]
-        return pl.ds(off - (pc.qkv if t < pc.early else pc.dn0), cw)
+        return pl.ds(off - pc.dn0 if t >= pc.early else off - (0 if mine else pc.qkv), cw)
 
     def own_pieces(t):
         refs = (pe_ref, te_ref) if t < pc.early else (pd_ref, td_ref)
-        return [ref.at[:, slim(t)] for ref in refs]
+        return [refs[0].at[:, slim(t, True)], refs[1].at[:, slim(t, False)]]
 
     def near_pieces(t, i):
-        return [(f0_ref, f1_ref)[i].at[:, slim(t)], tf_ref.at[i, :, slim(t)]]
+        return [(f0_ref, f1_ref)[i].at[:, slim(t, True)], tf_ref.at[i, :, slim(t, False)]]
 
     def stream():
         def cols(t):
@@ -507,9 +508,9 @@
                     remote(ref, ref, ps.at[t, i, h], wch.at[t], w.partner()).start()
                     sent.append((ref, ps.at[t, i, h]))
 
-        for s in range(2, n_chunk + far):
-            for h in range(far + 1):
-                hop(s - h, h)
+        for s in range(n_chunk + far):
+            for h in range(far, -1, -1):
+                hop(s - h if h > 1 else s + 1 - h, h)
         for ref, sem in sent:
             arrived(ref, sem)
         kvw = 2 * (kvb.shape[2] // 4)
@@ -529,11 +530,12 @@
             cp.start()
             sent.append(cp)
 
-        def load(t, dst, sem):
+        def load(t, dst, sem, first=True):
             off, cw = pc.chunks[t]
             c = pl.ds(off - pc.qkv, cw)
             near = t < pc.early
-            arrived(w_ref.at[pl.ds(0, n_fsdp - (6 if near else 2)), :, c], wch.at[t])
+            if first:
+                arrived(w_ref.at[pl.ds(0, n_fsdp - (6 if near else 2)), :, c], wch.at[t])
             for dz in range(-1, w.nz - 1):
                 two = pl.ds(2 * w.chip(dz), 2)
                 if dz == 0 or (near and dz in (1, -1)):
@@ -545,7 +547,7 @@
 
         own = [pltpu.make_async_copy(x_ref, xa.at[:, 0], lsem.at[0]),
                pltpu.make_async_copy(xb_ref, xa.at[0, 1], lsem.at[2]),
-               pltpu.make_async_copy(q_ref, wg.at[:, :, pl.ds(0, pc.qkv)], lsem.at[1])]
+               pltpu.make_async_copy(q_ref, wg.at[0, :, :, pl.ds(0, pc.qkv)], lsem.at[1])]
         for cp in own:
             cp.start()
         bits = [pl.ds(j * (seq // 2), seq // 2) for j in range(2)]
@@ -579,7 +581,7 @@
 
             def proj(nt, carry):
                 c = aligned(nt * 256, 256, LANES)
-                qf[:, c] = jnp.dot(mm[0], wg[:, :, c].reshape(width, 256), preferred_element_type=F32)
+                qf[:, c] = jnp.dot(mm[0], wg[0, :, :, c].reshape(width, 256), preferred_element_type=F32)
                 return carry
             lax.fori_loop(0, pc.qkv // 256, proj, 0)
 
@@ -675,10 +677,10 @@
         send_ctx(1, 1)
         relay_ctx(2, 1)
         relay_ctx(1, 1)
-        load(1, wd, lsem.at[0])
+        load(1, wd.at[0], lsem.at[0])
         for slot in range(4):
             send_kv(slot)
-        arrived(wd, lsem.at[0])
+        arrived(wd.at[0], lsem.at[0])
         n_ctx = len(sent)
 
         def mid(slot):
@@ -690,7 +692,7 @@
             def one(nt, carry):
                 c = aligned(nt * 256, 256, LANES)
                 o = aligned(w.me * pc.w4 + nt * 256, 256, LANES)
-                got = jnp.dot(ca[slot], wd[:, :, c].reshape(width, 256), preferred_element_type=F32)
+                got = jnp.dot(ca[slot], wd[0, :, :, c].reshape(width, 256), preferred_element_type=F32)
                 res = xa[slot, :, :, o].reshape(rows_b, 256).astype(F32)
                 xm[slot, :, o] = (res + got).astype(BF16)
                 return carry
@@ -708,49 +710,55 @@
         for cp in sent[:n_ctx]:
             cp.wait_send()
         del sent[:n_ctx]
-        for slot in (0, 2, 1, 3):
-            for q in (1, 2, 3):
-                if q == 3 or slot in (0, 2):
-                    take(xm, slot, q, ms_r)
-            norm_into(h2, slot, lambda rows, i, slot=slot: xm[slot, rows, :], g2_ref)
-
         gate_w = pc.gu_w // 2
-        for b in range(4):
-            load(2 + b, wg, lsem.at[b % 2])
-            arrived(wg, lsem.at[b % 2])
-
-            def one(j, carry):
-                s, nt = j // (gate_w // 256), j % (gate_w // 256)
-                act = h2[pl.ds(2 * s, 2)].reshape(2 * rows_b, width)
-                gate = jnp.dot(act, wg[:, :, aligned(nt * 256, 256, LANES)].reshape(width, 256), preferred_element_type=F32)
-                up = jnp.dot(act, wg[:, :, aligned(gate_w + nt * 256, 256, LANES)].reshape(width, 256), preferred_element_type=F32)
+        at = {0: 0, 2: 1, 1: 2, 3: 3}
+
+        def gate_up(group, b):
+            step = 4 * group + b
+            if step < 7:
+                load(2 + (b + 1) % 4, wg.at[(step + 1) % 2], lsem.at[1 + (step + 1) % 2], step < 3)
+            arrived(wg.at[step % 2], lsem.at[1 + step % 2])
+
+            def one(nt, carry):
+                act = h2[pl.ds(2 * group, 2)].reshape(2 * rows_b, width)
+                gate = jnp.dot(act, wg[step % 2, :, :, aligned(nt * 256, 256, LANES)].reshape(width, 256), preferred_element_type=F32)
+                up = jnp.dot(act, wg[step % 2, :, :, aligned(gate_w + nt * 256, 256, LANES)].reshape(width, 256), preferred_element_type=F32)
                 val = (jax.nn.silu(gate) * up).astype(BF16)
-                mm[pl.ds(2 * s, 2), :, aligned(b * gate_w + nt * 256, 256, LANES)] = val.reshape(2, rows_b, 256)
+                mm[pl.ds(2 * group, 2), :, aligned(b * gate_w + nt * 256, 256, LANES)] = val.reshape(2, rows_b, 256)
                 return carry
-            lax.fori_loop(0, 2 * (gate_w // 256), one, 0)
+            lax.fori_loop(0, gate_w // 256, one, 0)
+
+        load(2, wg.at[0], lsem.at[1])
+        for group, slots in enumerate(((0, 2), (1, 3))):
+            for slot in slots:
+                for q in (1, 2, 3):
+                    if q == 3 or slot in (0, 2):
+                        take(xm, slot, q, ms_r)
+                norm_into(h2, at[slot], lambda rows, i, slot=slot: xm[slot, rows, :], g2_ref)
+            for b in range(4):
+                gate_up(group, b)
 
         h0, h1 = pl.ds(0, half), pl.ds(half, half)
         first_sends, home = {}, []
 
         def phase1(n):
-            load(last_gu + 1 + n, wd, lsem.at[n % 2])
             for old in first_sends.get(n - 2, ()):
                 old.wait_send()
-            arrived(wd, lsem.at[n % 2])
             par = n % 2
+            arrived(wd.at[par], lsem.at[3 + par])
 
             def one(j, carry):
                 s, nt = j // (pc.dn_w // 256), j % (pc.dn_w // 256)
                 c = aligned(nt * 256, 256, LANES)
                 act = mm[pl.ds(2 * s, 2)].reshape(2 * rows_b, mm.shape[2])
-                got = jnp.dot(act, wd[:, :, c].reshape(mm.shape[2], 256), preferred_element_type=F32)
+                got = jnp.dot(act, wd[par, :, :, c].reshape(mm.shape[2], 256), preferred_element_type=F32)
                 pp[par, pl.ds(2 * s, 2), :, c] = got.reshape(2, rows_b, 256)
                 return carry
             lax.fori_loop(0, 2 * (pc.dn_w // 256), one, 0)
             first_sends[n] = []
             for path, dev, cc, rels in ((0, x, h0, (2, 3)), (1, y, h1, (1, 3))):
                 for j, rel in enumerate(rels):
-                    cp = remote(pp.at[par, rel, :, cc], r1.at[n, path, j], p1_s.at[n, path, j], p1_r.at[n, path, j], dev)
+                    cp = remote(pp.at[par, at[rel], :, cc], r1.at[n, path, j], p1_s.at[n, path, j], p1_r.at[n, path, j], dev)
                     cp.start()
                     first_sends[n].append(cp)
 
@@ -758,7 +766,7 @@
             par = n % 2
             for path, dev, cc, rel in ((0, y, h0, 1), (1, x, h1, 2)):
                 arrived(r1.at[n, path, 1], p1_r.at[n, path, 1])
-                r1[n, path, 1] = pp[par, rel, :, cc] + r1[n, path, 1]
+                r1[n, path, 1] = pp[par, at[rel], :, cc] + r1[n, path, 1]
                 go(remote(r1.at[n, path, 1], r2.at[n, path], p2_s.at[n, path], p2_r.at[n, path], dev))
             for path, cc in ((0, h0), (1, h1)):
                 arrived(r1.at[n, path, 0], p1_r.at[n, path, 0])
@@ -779,12 +787,18 @@
         for cp in sent:
             cp.wait_send()
         sent.clear()
+        def load_down(n):
+            load(last_gu + 1 + n, wd.at[n % 2], lsem.at[3 + n % 2])
+
+        load_down(0)
         for n in range(4):
             phase1(n)
             if n >= 1:
                 phase2(n - 1)
             if n >= 2:
                 phase3(n - 2)
+            if n < 3:
+                load_down(n + 1)
         phase2(3)
         phase3(2)
         phase3(3)
@@ -828,15 +842,15 @@
             pltpu.VMEM((4, 2, seq, width), BF16),
             pltpu.VMEM((4, rows_b, width), BF16),
             pltpu.VMEM((4, rows_b, width), BF16),
-            pltpu.VMEM((pc.n_fsdp, pc.rows, pc.gu_w), BF16),
-            pltpu.VMEM((pc.n_fsdp, pc.rows, pc.dn_w), BF16),
+            pltpu.VMEM((2, pc.n_fsdp, pc.rows, pc.gu_w), BF16),
+            pltpu.VMEM((2, pc.n_fsdp, pc.rows, pc.dn_w), BF16),
             pltpu.VMEM((4, rows_b, max(ff4, width)), BF16),
             pltpu.VMEM((2, 4, rows_b, pc.dn_w), F32),
             pltpu.VMEM((4, 2, 2, rows_b, half), F32),
             pltpu.VMEM((4, 2, rows_b, half), F32),
             pltpu.VMEM((rows_b, pc.qkv), F32),
             pltpu.VMEM((4, rows_b, 2 * pc.kv4), BF16),
-            dma((3,)),
+            dma((5,)),
             dma((6,)), dma((4, 2)),
             dma((4, 2, 3)), dma((4, 2, 3)),
             dma((4, 3)), dma((4, 3)),
@@ -868,11 +882,10 @@
         pc = Pieces(rows, q_width // 4, kv_width // 4, width // 4, w_down.shape[0] // 4, n_fsdp, width)
 
         gains = jnp.stack([norm_attn, norm_mlp]).astype(F32)
-        ids, gains, pq, pe, pd = gather_ids(side, pc, tokens, gains, w_qkv, w_out, w_gate_up, w_down)
+        ids, gains, pe, pd = gather_ids(side, pc, tokens, gains, w_qkv, w_out, w_gate_up, w_down)
         def first_hop(piece, dz):
             return lax.ppermute(piece, 'fsdp', [(i, (i + 2 * dz) % n_fsdp) for i in range(n_fsdp)])
 
-        n0, n1 = first_hop(pq, 1), first_hop(pq, -1)
         f0, f1 = first_hop(pe, 1), first_hop(pe, -1)
         ids = ids.reshape(-1) - lax.axis_index('fsdp') * shard_rows
         owned = (ids >= 0) & (ids < shard_rows)
@@ -889,7 +902,7 @@
         sin_tab = jnp.concatenate([-sin_tab, sin_tab] * reps, axis=1)
 
         table_rows = table_rows.reshape(n_fsdp // 2, 2, seq, width)
-        x, xb, q_all, te, td, tf = embed(side, pc, table_rows, pq, n0, n1, pe, pd, f0, f1)
+        x, xb, q_all, te, td, tf = embed(side, pc, table_rows, pe, pd, f0, f1)
         out, k, v, _ = layer(side, pc, head_dim, x, xb, q_all, (pe, pd, f0, f1, te, td, tf), g1, g2, cos_tab, sin_tab)
         heads = (1, seq, kv_width // head_dim, head_dim)
         return out[None], k.reshape(heads), v.reshape(heads)

time: 278 us -> 280 us (level)
  Pallas kernels: 259 us -> 264 us
    pallas_call x1, Pallas kernels: 145 us -> 150 us  [layer(): pl.pallas_call(functools.partial(layer_kernel, side, pc, head_dim), out_s...]
  transfers between devices with their start and end apart: 4 -> 2, of which waited for: 0 -> 0; matrix products, arithmetic and copies ran while one was open for 2% -> 1% of each run, Pallas kernels for 11% -> 11%
where the time goes in v1:
time: 280 us; the launch traced here: 278 us
  Pallas kernels  264 us (94%)
  local copies, waits for them, and re-layouts  6.2 us (2%)
  other arithmetic  4.41 us (2%)
    pallas_call x1, Pallas kernels, layer(): pl.pallas_call(functools.partial(layer_kernel, side, pc, head_dim), out_s...  150 us
    pallas_call x1, Pallas kernels, embed(): pl.pallas_call(functools.partial(embed_kernel, side, pc), out_shape=(jax....  67.9 us
    pallas_call x1, Pallas kernels, gather_table(): pl.pallas_call(functools.partial(gather_kernel, n_tok), out_shape=jax.Sha...  30.2 us
    pallas_call x1, Pallas kernels, gather_ids(): pl.pallas_call(functools.partial(ids_kernel, side, pc), out_shape=(jax.Sh...  15.6 us
  transfers between devices with their start and end apart: 2, of which 0 were waited for; matrix products, arithmetic and copies ran while one was open for 1% of the time, Pallas kernels for 11%

profile of v1, /device:TPU:21, one launch (start us, length us, event | category | flops | bytes accessed | tf_op | source)
XLA Modules:
  0.0 277.7 jit_solution(6971048043649599681)
XLA Ops:
  0.6 1.2 maximum_convert_fusion.gain_ref
  1.9 15.6 %ids.1 = (s32[16,1,128]{2,1,0:T(1,128)}, f32[16,2,128]{2,1,0:T(2,128)}, bf16[128,5376]{1,0:T(8,128)(2,1)}, bf16[128,2048]{1,0:T(8,128)(2,1)}) custom-call(s32[1,128]{1,0:T(1,128)} %tok_ref.1, f32[2,128]{1,0:T(2,128)} %maximum_convert_fusion.gain_ref, bf16[128,3072]{1,0:T(8,128)(2,1)} %w_qkv.1, bf16[128,2048]{1,0:T(8,128)(2,1)} %w_out.1, ...), custom_call_target="tpu_custom_call" | custom-call | tf_op jit(solution)/shard_map/ids/pallas_call | solution.py:144
  17.5 2.2 collective-permute-start.1
  19.7 0.0 collective-permute-start
  19.7 0.7 fusion.16
  20.4 0.7 broadcast_subtract_fusion
  21.1 0.4 copy.14
  21.5 0.6 fusion.2.tgt_ref
  22.1 0.0 copy-start.1
  22.1 0.0 copy-start
  22.2 30.2 %rows.1 = bf16[2048,2048]{1,0:T(8,128)(2,1)} custom-call(s32[2048]{0:T(1024)S(1)} %fusion.11.gid_ref, s32[2048,1]{1,0:T(8,128)S(1)} %fusion.2.tgt_ref, bf16[1002,8,2048]{2,1,0:T(8,128)(2,1)} %bitcast.24), custom_call_target="tpu_custom_call" | custom-call | flops 80000000000 | bytes 75497472 | tf_op jit(solution)/shard_map/rows/pallas_call | solution.py:191
  52.4 0.0 copy-done.1
  52.4 0.3 fusion.9
  52.7 0.8 pad_maximum_fusion
  53.5 0.0 copy-done
  53.5 0.6 slice_bitcast_fusion
  54.1 0.0 collective-permute-done.1.f1_ref
  54.1 0.0 collective-permute-done.f0_ref
  54.1 67.9 %embed.1 = (bf16[4,128,2048]{2,1,0:T(8,128)(2,1)}, bf16[128,2048]{1,0:T(8,128)(2,1)}, bf16[16,128,768]{2,1,0:T(8,128)(2,1)}, bf16[128,4608]{1,0:T(8,128)(2,1)}, ...) custom-call(bf16[8,2,128,2048]{3,2,1,0:T(8,128)(2,1)} %bitcast.16, bf16[128,5376]{1,0:T(8,128)(2,1)} %get-tuple-element.17.pe_ref, ...), custom_call_target="tpu_custom_call" | custom-call | tf_op jit(solution)/shard_map/embed/pallas_call | solution.py:413
  122.0 150.5 %layer.1 = (bf16[128,2048]{1,0:T(8,128)(2,1)}, bf16[128,512]{1,0:T(8,128)(2,1)}, bf16[128,512]{1,0:T(8,128)(2,1)}, bf16[16,128,6656]{2,1,0:T(8,128)(2,1)}) custom-call(bf16[4,128,2048]{2,1,0:T(8,128)(2,1)} %get-tuple-element.19.x_ref, bf16[128,2048]{1,0:T(8,128)(2,1)} %get-tuple-element.20.xb_ref, bf16[16,128,768]{2,1,0:T(8,128)(2,1)} %get-tuple-element.21.q_ref, ...), custom_call_target="tpu_custom_call" | custom-call | tf_op jit(solution)/shard_map/layer/pallas_call | solution.py:832
  272.5 1.7 copy.19
  274.2 1.7 copy.20
  275.8 1.9 copy.22
  (2 shorter events, 0.0 us)
Async XLA Ops:
  17.5 36.6 %collective-permute-start.1 = (bf16[128,5376]{1,0:T(8,128)(2,1)}, bf16[128,5376]{1,0:T(8,128)(2,1)}, u32[]{:S(2)}, u32[]{:S(2)}) collective-permute-start(bf16[128,5376]{1,0:T(8,128)(2,1)} %get-tuple-element.17.pe_ref), channel_id=1, source_target_pairs={{0,14},{1,15},{2,0},{3,1},{4,2},{5,3},{6,4},{7,5},{8,6},{9,7},{10,... | collective-permute-start | bytes 4128776 | tf_op jit(solution)/shard_map/ppermute | solution.py:887
  19.7 34.4 %collective-permute-start = (bf16[128,5376]{1,0:T(8,128)(2,1)}, bf16[128,5376]{1,0:T(8,128)(2,1)}, u32[]{:S(2)}, u32[]{:S(2)}) collective-permute-start(bf16[128,5376]{1,0:T(8,128)(2,1)} %get-tuple-element.17.pe_ref), channel_id=1, source_target_pairs={{0,2},{1,3},{2,4},{3,5},{4,6},{5,7},{6,8},{7,9},{8,10},{9,11},{10,... | collective-permute-start | bytes 4128776 | tf_op jit(solution)/shard_map/ppermute | solution.py:887
  22.1 30.2 %copy-start.1 = (f32[32]{0:T(128)S(1)}, f32[32]{0:T(128)}, u32[]{:S(2)}) copy-start(f32[32]{0:T(128)} %param.17) | copy-start | bytes 388
  22.1 31.4 %copy-start = (f32[16,2,128]{2,1,0:T(2,128)S(1)}, f32[16,2,128]{2,1,0:T(2,128)}, u32[]{:S(2)}) copy-start(f32[16,2,128]{2,1,0:T(2,128)} %get-tuple-element.25) | copy-start | bytes 49156

commit v2 on v1

--- a/solution.py
+++ b/solution.py
@@ -108,12 +108,13 @@
         self.gu0 = self.qkv + w4
         self.gu_w = 2 * f4 * n_fsdp // 4
         self.dn0 = self.gu0 + 4 * self.gu_w
-        self.dn_w = width // 4
+        self.n_dn = 8
+        self.dn_w = width // self.n_dn
         self.total = self.dn0 + width
         self.late = self.total - self.qkv
         self.chunks = [(0, self.qkv), (self.qkv, w4)]
         self.chunks += [(self.gu0 + b * self.gu_w, self.gu_w) for b in range(4)]
-        self.chunks += [(self.dn0 + n * self.dn_w, self.dn_w) for n in range(4)]
+        self.chunks += [(self.dn0 + n * self.dn_w, self.dn_w) for n in range(self.n_dn)]
         self.early = 6
 
 
@@ -517,7 +518,7 @@
         for rel in range(4):
             arrived(k_ref.at[:, pl.ds(0, kvw)], kv_r.at[rel, 0])
             arrived(v_ref.at[:, pl.ds(0, kvw)], kv_r.at[rel, 1])
-        for n in range(4):
+        for n in range(pc.n_dn):
             arrived(out_ref.at[:, pl.ds(n * pc.dn_w, pc.dn_w)], o_r.at[n])
 
     def compute():
@@ -714,29 +715,46 @@
         at = {0: 0, 2: 1, 1: 2, 3: 3}
 
         def gate_up(group, b):
-            step = 4 * group + b
-            if step < 7:
-                load(2 + (b + 1) % 4, wg.at[(step + 1) % 2], lsem.at[1 + (step + 1) % 2], step < 3)
-            arrived(wg.at[step % 2], lsem.at[1 + step % 2])
-
             def one(nt, carry):
                 act = h2[pl.ds(2 * group, 2)].reshape(2 * rows_b, width)
-                gate = jnp.dot(act, wg[step % 2, :, :, aligned(nt * 256, 256, LANES)].reshape(width, 256), preferred_element_type=F32)
-                up = jnp.dot(act, wg[step % 2, :, :, aligned(gate_w + nt * 256, 256, LANES)].reshape(width, 256), preferred_element_type=F32)
+                gate = jnp.dot(act, wg[b % 2, :, :, aligned(nt * 256, 256, LANES)].reshape(width, 256), preferred_element_type=F32)
+                up = jnp.dot(act, wg[b % 2, :, :, aligned(gate_w + nt * 256, 256, LANES)].reshape(width, 256), preferred_element_type=F32)
                 val = (jax.nn.silu(gate) * up).astype(BF16)
                 mm[pl.ds(2 * group, 2), :, aligned(b * gate_w + nt * 256, 256, LANES)] = val.reshape(2, rows_b, 256)
                 return carry
             lax.fori_loop(0, gate_w // 256, one, 0)
 
-        load(2, wg.at[0], lsem.at[1])
-        for group, slots in enumerate(((0, 2), (1, 3))):
-            for slot in slots:
+        def load_gate(b):
+            load(2 + b, wg.at[b % 2], lsem.at[1 + b % 2])
+
+        def gate_here(b):
+            arrived(wg.at[b % 2], lsem.at[1 + b % 2])
+
+        def normed(group):
+            for slot in ((0, 2), (1, 3))[group]:
                 for q in (1, 2, 3):
                     if q == 3 or slot in (0, 2):
                         take(xm, slot, q, ms_r)
-                norm_into(h2, at[slot], lambda rows, i, slot=slot: xm[slot, rows, :], g2_ref)
-            for b in range(4):
-                gate_up(group, b)
+                norm_into(h2, at[slot], lambda rows, i: xm[slot, rows, :], g2_ref)
+
+        load_gate(0)
+        normed(0)
+        gate_here(0)
+        gate_up(0, 0)
+        load_gate(1)
+        normed(1)
+        gate_up(1, 0)
+        load_gate(2)
+        gate_here(1)
+        gate_up(0, 1)
+        gate_up(1, 1)
+        gate_here(2)
+        gate_up(0, 2)
+        gate_up(1, 2)
+        load_gate(3)
+        gate_here(3)
+        gate_up(0, 3)
+        gate_up(1, 3)
 
         h0, h1 = pl.ds(0, half), pl.ds(half, half)
         first_sends, home = {}, []
@@ -745,7 +763,7 @@
             for old in first_sends.get(n - 2, ()):
                 old.wait_send()
             par = n % 2
-            arrived(wd.at[par], lsem.at[3 + par])
+            arrived(wd.at[par, :, :, pl.ds(0, pc.dn_w)], lsem.at[3 + par])
 
             def one(j, carry):
                 s, nt = j // (pc.dn_w // 256), j % (pc.dn_w // 256)
@@ -788,24 +806,25 @@
             cp.wait_send()
         sent.clear()
         def load_down(n):
-            load(last_gu + 1 + n, wd.at[n % 2], lsem.at[3 + n % 2])
+            load(last_gu + 1 + n, wd.at[n % 2, :, :, pl.ds(0, pc.dn_w)], lsem.at[3 + n % 2])
 
         load_down(0)
-        for n in range(4):
+        last = pc.n_dn - 1
+        for n in range(pc.n_dn):
             phase1(n)
             if n >= 1:
                 phase2(n - 1)
             if n >= 2:
                 phase3(n - 2)
-            if n < 3:
+            if n < last:
                 load_down(n + 1)
-        phase2(3)
-        phase3(2)
-        phase3(3)
+        phase2(last)
+        phase3(last - 1)
+        phase3(last)
 
         for cp in sent:
             cp.wait_send()
-        for n in (2, 3):
+        for n in (last - 1, last):
             for cp in first_sends[n]:
                 cp.wait_send()
         for cp in local_kv + home:
@@ -843,11 +862,11 @@
             pltpu.VMEM((4, rows_b, width), BF16),
             pltpu.VMEM((4, rows_b, width), BF16),
             pltpu.VMEM((2, pc.n_fsdp, pc.rows, pc.gu_w), BF16),
-            pltpu.VMEM((2, pc.n_fsdp, pc.rows, pc.dn_w), BF16),
+            pltpu.VMEM((2, pc.n_fsdp, pc.rows, pc.w4), BF16),
             pltpu.VMEM((4, rows_b, max(ff4, width)), BF16),
             pltpu.VMEM((2, 4, rows_b, pc.dn_w), F32),
-            pltpu.VMEM((4, 2, 2, rows_b, half), F32),
-            pltpu.VMEM((4, 2, rows_b, half), F32),
+            pltpu.VMEM((pc.n_dn, 2, 2, rows_b, half), F32),
+            pltpu.VMEM((pc.n_dn, 2, rows_b, half), F32),
             pltpu.VMEM((rows_b, pc.qkv), F32),
             pltpu.VMEM((4, rows_b, 2 * pc.kv4), BF16),
             dma((5,)),
@@ -855,9 +874,9 @@
             dma((4, 2, 3)), dma((4, 2, 3)),
             dma((4, 3)), dma((4, 3)),
             dma((4, 2, 2)), dma((4, 2)),
-            dma((4, 2, 2)), dma((4, 2, 2)),
-            dma((4, 2)), dma((4, 2)),
-            dma((4,)), dma((4,)), dma((4,)),
+            dma((pc.n_dn, 2, 2)), dma((pc.n_dn, 2, 2)),
+            dma((pc.n_dn, 2)), dma((pc.n_dn, 2)),
+            dma((pc.n_dn,)), dma((pc.n_dn,)), dma((pc.n_dn,)),
             dma((n_chunk, 2, far + 1)), dma((n_chunk, 2, far + 1)), dma((n_chunk, 2, far + 1)), dma((n_chunk,)),
         ],
         compiler_params=pltpu.CompilerParams(collective_id=2, has_side_effects=True, vmem_limit_bytes=67043328),

time: 280 us -> 267 us (0.954)
  Pallas kernels: 264 us -> 251 us
    pallas_call x1, Pallas kernels: 150 us -> 137 us  [layer(): pl.pallas_call(functools.partial(layer_kernel, side, pc, head_dim), out_s...]
  transfers between devices with their start and end apart: 2 -> 2, of which waited for: 0 -> 0; matrix products, arithmetic and copies ran while one was open for 1% -> 2% of each run, Pallas kernels for 11% -> 12%
where the time goes in v2:
time: 267 us; the launch traced here: 264 us
  Pallas kernels  251 us (94%)
  local copies, waits for them, and re-layouts  6.2 us (2%)
  other arithmetic  4.41 us (2%)
    pallas_call x1, Pallas kernels, layer(): pl.pallas_call(functools.partial(layer_kernel, side, pc, head_dim), out_s...  137 us
    pallas_call x1, Pallas kernels, embed(): pl.pallas_call(functools.partial(embed_kernel, side, pc), out_shape=(jax....  67.5 us
    pallas_call x1, Pallas kernels, gather_table(): pl.pallas_call(functools.partial(gather_kernel, n_tok), out_shape=jax.Sha...  30.7 us
    pallas_call x1, Pallas kernels, gather_ids(): pl.pallas_call(functools.partial(ids_kernel, side, pc), out_shape=(jax.Sh...  15.6 us
  transfers between devices with their start and end apart: 2, of which 0 were waited for; matrix products, arithmetic and copies ran while one was open for 2% of the time, Pallas kernels for 12%

profile of v2, /device:TPU:21, one launch (start us, length us, event | category | flops | bytes accessed | tf_op | source)
XLA Modules:
  0.0 264.1 jit_solution(8916366260215262990)
XLA Ops:
  0.6 1.2 maximum_convert_fusion.gain_ref
  1.9 15.6 %ids.1 = (s32[16,1,128]{2,1,0:T(1,128)}, f32[16,2,128]{2,1,0:T(2,128)}, bf16[128,5376]{1,0:T(8,128)(2,1)}, bf16[128,2048]{1,0:T(8,128)(2,1)}) custom-call(s32[1,128]{1,0:T(1,128)} %tok_ref.1, f32[2,128]{1,0:T(2,128)} %maximum_convert_fusion.gain_ref, bf16[128,3072]{1,0:T(8,128)(2,1)} %w_qkv.1, bf16[128,2048]{1,0:T(8,128)(2,1)} %w_out.1, ...), custom_call_target="tpu_custom_call" | custom-call | tf_op jit(solution)/shard_map/ids/pallas_call | solution.py:145
  17.5 2.2 collective-permute-start.1
  19.7 0.0 collective-permute-start
  19.7 0.7 fusion.16
  20.4 0.7 broadcast_subtract_fusion
  21.1 0.4 copy.14
  21.5 0.6 fusion.2.tgt_ref
  22.1 0.0 copy-start.1
  22.1 0.0 copy-start
  22.2 30.7 %rows.1 = bf16[2048,2048]{1,0:T(8,128)(2,1)} custom-call(s32[2048]{0:T(1024)S(1)} %fusion.11.gid_ref, s32[2048,1]{1,0:T(8,128)S(1)} %fusion.2.tgt_ref, bf16[1002,8,2048]{2,1,0:T(8,128)(2,1)} %bitcast.24), custom_call_target="tpu_custom_call" | custom-call | flops 80000000000 | bytes 75497472 | tf_op jit(solution)/shard_map/rows/pallas_call | solution.py:192
  52.8 0.0 copy-done.1
  52.9 0.3 fusion.9
  53.1 0.8 pad_maximum_fusion
  53.9 0.0 copy-done
  53.9 0.6 slice_bitcast_fusion
  54.6 0.0 collective-permute-done.1.f1_ref
  54.6 0.0 collective-permute-done.f0_ref
  54.6 67.5 %embed.1 = (bf16[4,128,2048]{2,1,0:T(8,128)(2,1)}, bf16[128,2048]{1,0:T(8,128)(2,1)}, bf16[16,128,768]{2,1,0:T(8,128)(2,1)}, bf16[128,4608]{1,0:T(8,128)(2,1)}, ...) custom-call(bf16[8,2,128,2048]{3,2,1,0:T(8,128)(2,1)} %bitcast.16, bf16[128,5376]{1,0:T(8,128)(2,1)} %get-tuple-element.17.pe_ref, ...), custom_call_target="tpu_custom_call" | custom-call | tf_op jit(solution)/shard_map/embed/pallas_call | solution.py:414
  122.0 136.8 %layer.1 = (bf16[128,2048]{1,0:T(8,128)(2,1)}, bf16[128,512]{1,0:T(8,128)(2,1)}, bf16[128,512]{1,0:T(8,128)(2,1)}, bf16[16,128,6656]{2,1,0:T(8,128)(2,1)}) custom-call(bf16[4,128,2048]{2,1,0:T(8,128)(2,1)} %get-tuple-element.19.x_ref, bf16[128,2048]{1,0:T(8,128)(2,1)} %get-tuple-element.20.xb_ref, bf16[16,128,768]{2,1,0:T(8,128)(2,1)} %get-tuple-element.21.q_ref, ...), custom_call_target="tpu_custom_call" | custom-call | tf_op jit(solution)/shard_map/layer/pallas_call | solution.py:851
  258.8 1.7 copy.19
  260.5 1.7 copy.20
  262.2 1.9 copy.22
  (2 shorter events, 0.0 us)
Async XLA Ops:
  17.5 37.1 %collective-permute-start.1 = (bf16[128,5376]{1,0:T(8,128)(2,1)}, bf16[128,5376]{1,0:T(8,128)(2,1)}, u32[]{:S(2)}, u32[]{:S(2)}) collective-permute-start(bf16[128,5376]{1,0:T(8,128)(2,1)} %get-tuple-element.17.pe_ref), channel_id=1, source_target_pairs={{0,14},{1,15},{2,0},{3,1},{4,2},{5,3},{6,4},{7,5},{8,6},{9,7},{10,... | collective-permute-start | bytes 4128776 | tf_op jit(solution)/shard_map/ppermute | solution.py:906
  19.7 34.9 %collective-permute-start = (bf16[128,5376]{1,0:T(8,128)(2,1)}, bf16[128,5376]{1,0:T(8,128)(2,1)}, u32[]{:S(2)}, u32[]{:S(2)}) collective-permute-start(bf16[128,5376]{1,0:T(8,128)(2,1)} %get-tuple-element.17.pe_ref), channel_id=1, source_target_pairs={{0,2},{1,3},{2,4},{3,5},{4,6},{5,7},{6,8},{7,9},{8,10},{9,11},{10,... | collective-permute-start | bytes 4128776 | tf_op jit(solution)/shard_map/ppermute | solution.py:906
  22.1 30.7 %copy-start.1 = (f32[32]{0:T(128)S(1)}, f32[32]{0:T(128)}, u32[]{:S(2)}) copy-start(f32[32]{0:T(128)} %param.17) | copy-start | bytes 388
  22.1 31.8 %copy-start = (f32[16,2,128]{2,1,0:T(2,128)S(1)}, f32[16,2,128]{2,1,0:T(2,128)}, u32[]{:S(2)}) copy-start(f32[16,2,128]{2,1,0:T(2,128)} %get-tuple-element.25) | copy-start | bytes 49156

commit v3 on v2

--- a/solution.py
+++ b/solution.py
@@ -659,6 +659,23 @@
             for slot in ((2, 0) if q == 2 else (0, 2)):
                 relay(ca, slot, q, cs_s, cs_r, seqs[h], (h,))
 
+        def mid(slot, h):
+            for q in (1, 2, 3):
+                if q == 3 or slot in (1, 3):
+                    take(ca, slot, q, cs_r, seqs[h], (h,))
+
+            def one(nt, carry):
+                c = aligned(nt * 256, 256, LANES)
+                o = aligned(w.me * pc.w4 + nt * 256, 256, LANES)
+                got = jnp.dot(ca[slot, seqs[h], :], wd[0, :, :, c].reshape(width, 256), preferred_element_type=F32)
+                xm[slot, seqs[h], o] = (xa[slot, h, :, o].astype(F32) + got).astype(BF16)
+                return carry
+            lax.fori_loop(0, pc.w4 // 256, one, 0)
+            spread(xm, slot, ms_s, ms_r, seqs[h], (h,))
+
+        def relay_mid(slot, q, h):
+            relay(xm, slot, q, ms_s, ms_r, seqs[h], (h,))
+
         attend(0, 0)
         send_ctx(0, 0)
         here(2, 0)
@@ -677,37 +694,23 @@
         attend(1, 1)
         send_ctx(1, 1)
         relay_ctx(2, 1)
+        load(1, wd.at[0], lsem.at[0])
+        arrived(wd.at[0], lsem.at[0])
+        for slot in (3, 1, 2, 0):
+            mid(slot, 0)
         relay_ctx(1, 1)
-        load(1, wd.at[0], lsem.at[0])
         for slot in range(4):
             send_kv(slot)
-        arrived(wd.at[0], lsem.at[0])
         n_ctx = len(sent)
 
-        def mid(slot):
-            for q in (1, 2, 3):
-                if q == 3 or slot in (1, 3):
-                    for h in range(2):
-                        take(ca, slot, q, cs_r, seqs[h], (h,))
-
-            def one(nt, carry):
-                c = aligned(nt * 256, 256, LANES)
-                o = aligned(w.me * pc.w4 + nt * 256, 256, LANES)
-                got = jnp.dot(ca[slot], wd[0, :, :, c].reshape(width, 256), preferred_element_type=F32)
-                res = xa[slot, :, :, o].reshape(rows_b, 256).astype(F32)
-                xm[slot, :, o] = (res + got).astype(BF16)
-                return carry
-            lax.fori_loop(0, pc.w4 // 256, one, 0)
-            spread(xm, slot, ms_s, ms_r)
-
-        mid(3)
-        mid(1)
-        mid(2)
-        relay(xm, 1, 2, ms_s, ms_r)
-        mid(0)
-        relay(xm, 3, 2, ms_s, ms_r)
-        relay(xm, 3, 1, ms_s, ms_r)
-        relay(xm, 1, 1, ms_s, ms_r)
+        mid(3, 1)
+        mid(1, 1)
+        for slot, q in ((1, 2), (3, 2), (3, 1), (1, 1)):
+            relay_mid(slot, q, 0)
+        mid(2, 1)
+        mid(0, 1)
+        for slot, q in ((1, 2), (3, 2), (3, 1), (1, 1)):
+            relay_mid(slot, q, 1)
         for cp in sent[:n_ctx]:
             cp.wait_send()
         del sent[:n_ctx]
@@ -734,7 +737,8 @@
             for slot in ((0, 2), (1, 3))[group]:
                 for q in (1, 2, 3):
                     if q == 3 or slot in (0, 2):
-                        take(xm, slot, q, ms_r)
+                        for h in range(2):
+                            take(xm, slot, q, ms_r, seqs[h], (h,))
                 norm_into(h2, at[slot], lambda rows, i: xm[slot, rows, :], g2_ref)
 
         load_gate(0)
@@ -872,7 +876,7 @@
             dma((5,)),
             dma((6,)), dma((4, 2)),
             dma((4, 2, 3)), dma((4, 2, 3)),
-            dma((4, 3)), dma((4, 3)),
+            dma((4, 2, 3)), dma((4, 2, 3)),
             dma((4, 2, 2)), dma((4, 2)),
             dma((pc.n_dn, 2, 2)), dma((pc.n_dn, 2, 2)),
             dma((pc.n_dn, 2)), dma((pc.n_dn, 2)),

time: 267 us -> 266 us (level)
  no operation moved by 1% of the time
where the time goes in v3:
time: 266 us; the launch traced here: 264 us
  Pallas kernels  250 us (94%)
  local copies, waits for them, and re-layouts  6.2 us (2%)
  other arithmetic  4.41 us (2%)
    pallas_call x1, Pallas kernels, layer(): pl.pallas_call(functools.partial(layer_kernel, side, pc, head_dim), out_s...  137 us
    pallas_call x1, Pallas kernels, embed(): pl.pallas_call(functools.partial(embed_kernel, side, pc), out_shape=(jax....  67.4 us
    pallas_call x1, Pallas kernels, gather_table(): pl.pallas_call(functools.partial(gather_kernel, n_tok), out_shape=jax.Sha...  30.7 us
    pallas_call x1, Pallas kernels, gather_ids(): pl.pallas_call(functools.partial(ids_kernel, side, pc), out_shape=(jax.Sh...  15.6 us
  transfers between devices with their start and end apart: 2, of which 0 were waited for; matrix products, arithmetic and copies ran while one was open for 2% of the time, Pallas kernels for 12%

profile of v3, /device:TPU:21, one launch (start us, length us, event | category | flops | bytes accessed | tf_op | source)
XLA Modules:
  0.0 263.9 jit_solution(7027844232512828373)
XLA Ops:
  0.6 1.2 maximum_convert_fusion.gain_ref
  1.9 15.6 %ids.1 = (s32[16,1,128]{2,1,0:T(1,128)}, f32[16,2,128]{2,1,0:T(2,128)}, bf16[128,5376]{1,0:T(8,128)(2,1)}, bf16[128,2048]{1,0:T(8,128)(2,1)}) custom-call(s32[1,128]{1,0:T(1,128)} %tok_ref.1, f32[2,128]{1,0:T(2,128)} %maximum_convert_fusion.gain_ref, bf16[128,3072]{1,0:T(8,128)(2,1)} %w_qkv.1, bf16[128,2048]{1,0:T(8,128)(2,1)} %w_out.1, ...), custom_call_target="tpu_custom_call" | custom-call | tf_op jit(solution)/shard_map/ids/pallas_call | solution.py:145
  17.5 2.2 collective-permute-start.1
  19.7 0.0 collective-permute-start
  19.7 0.7 fusion.16
  20.4 0.7 broadcast_subtract_fusion
  21.1 0.4 copy.14
  21.5 0.6 fusion.2.tgt_ref
  22.1 0.0 copy-start.1
  22.1 0.0 copy-start
  22.2 30.7 %rows.1 = bf16[2048,2048]{1,0:T(8,128)(2,1)} custom-call(s32[2048]{0:T(1024)S(1)} %fusion.11.gid_ref, s32[2048,1]{1,0:T(8,128)S(1)} %fusion.2.tgt_ref, bf16[1002,8,2048]{2,1,0:T(8,128)(2,1)} %bitcast.24), custom_call_target="tpu_custom_call" | custom-call | flops 80000000000 | bytes 75497472 | tf_op jit(solution)/shard_map/rows/pallas_call | solution.py:192
  52.8 0.0 copy-done.1
  52.9 0.3 fusion.9
  53.1 0.8 pad_maximum_fusion
  54.0 0.0 copy-done
  54.0 0.6 slice_bitcast_fusion
  54.6 0.0 collective-permute-done.1.f1_ref
  54.6 0.0 collective-permute-done.f0_ref
  54.6 67.4 %embed.1 = (bf16[4,128,2048]{2,1,0:T(8,128)(2,1)}, bf16[128,2048]{1,0:T(8,128)(2,1)}, bf16[16,128,768]{2,1,0:T(8,128)(2,1)}, bf16[128,4608]{1,0:T(8,128)(2,1)}, ...) custom-call(bf16[8,2,128,2048]{3,2,1,0:T(8,128)(2,1)} %bitcast.16, bf16[128,5376]{1,0:T(8,128)(2,1)} %get-tuple-element.17.pe_ref, ...), custom_call_target="tpu_custom_call" | custom-call | tf_op jit(solution)/shard_map/embed/pallas_call | solution.py:414
  122.0 136.7 %layer.1 = (bf16[128,2048]{1,0:T(8,128)(2,1)}, bf16[128,512]{1,0:T(8,128)(2,1)}, bf16[128,512]{1,0:T(8,128)(2,1)}, bf16[16,128,6656]{2,1,0:T(8,128)(2,1)}) custom-call(bf16[4,128,2048]{2,1,0:T(8,128)(2,1)} %get-tuple-element.19.x_ref, bf16[128,2048]{1,0:T(8,128)(2,1)} %get-tuple-element.20.xb_ref, bf16[16,128,768]{2,1,0:T(8,128)(2,1)} %get-tuple-element.21.q_ref, ...), custom_call_target="tpu_custom_call" | custom-call | tf_op jit(solution)/shard_map/layer/pallas_call | solution.py:855
  258.7 1.7 copy.19
  260.4 1.7 copy.20
  262.0 1.9 copy.22
  (2 shorter events, 0.0 us)
Async XLA Ops:
  17.5 37.1 %collective-permute-start.1 = (bf16[128,5376]{1,0:T(8,128)(2,1)}, bf16[128,5376]{1,0:T(8,128)(2,1)}, u32[]{:S(2)}, u32[]{:S(2)}) collective-permute-start(bf16[128,5376]{1,0:T(8,128)(2,1)} %get-tuple-element.17.pe_ref), channel_id=1, source_target_pairs={{0,14},{1,15},{2,0},{3,1},{4,2},{5,3},{6,4},{7,5},{8,6},{9,7},{10,... | collective-permute-start | bytes 4128776 | tf_op jit(solution)/shard_map/ppermute | solution.py:910
  19.7 34.9 %collective-permute-start = (bf16[128,5376]{1,0:T(8,128)(2,1)}, bf16[128,5376]{1,0:T(8,128)(2,1)}, u32[]{:S(2)}, u32[]{:S(2)}) collective-permute-start(bf16[128,5376]{1,0:T(8,128)(2,1)} %get-tuple-element.17.pe_ref), channel_id=1, source_target_pairs={{0,2},{1,3},{2,4},{3,5},{4,6},{5,7},{6,8},{7,9},{8,10},{9,11},{10,... | collective-permute-start | bytes 4128776 | tf_op jit(solution)/shard_map/ppermute | solution.py:910
  22.1 30.7 %copy-start.1 = (f32[32]{0:T(128)S(1)}, f32[32]{0:T(128)}, u32[]{:S(2)}) copy-start(f32[32]{0:T(128)} %param.17) | copy-start | bytes 388
  22.1 31.8 %copy-start = (f32[16,2,128]{2,1,0:T(2,128)S(1)}, f32[16,2,128]{2,1,0:T(2,128)}, u32[]{:S(2)}) copy-start(f32[16,2,128]{2,1,0:T(2,128)} %get-tuple-element.25) | copy-start | bytes 49156
